TPU v7x, 256 devices: a whole 4x4x8 slice. The times are simulated.
256 devices in a mesh: region: 16 (over z, x_hi), feat: 4 (over x_lo, core), row: 4 (over y).
Axes of the slice: x: 4 (x_hi: 2, x_lo: 2; x = x_hi * 2 + x_lo), y: 4, z: 8, core: 2. Of those that a mesh axis runs over, the one named last changes fastest.
Arguments:
- samples: bfloat16 [524288, 128], P(('region', 'row')), may hold values from -6 to 6
- targets: bfloat16 [524288, 64], P(('region', 'row')), may hold values from -6 to 6
- member: int32 [524288], P(('region', 'row')), may hold values 0 or 1
- omega: bfloat16 [128, 4096], P(None, 'feat'), may hold values from -0.5 to 0.5
- phase: float32 [4096], P('feat'), may hold values from -3.140625 to 3.140625
- factors: float32 [65536, 1024], P(('region', 'feat')), may hold values from -0.08 to 5, as said below
- weights_init: float32 [65536, 64], P(('region', 'feat'), 'row'), may hold values from -3 to 3
- duals_init: float32 [65536, 64], P(('region', 'feat'), 'row'), may hold values from -2 to 2
- consensus_init: float32 [4096, 64], P('feat', 'row'), may hold values from -3 to 3
- penalty_init: float32 [16], P('region'), may hold values from 2 to 8
Outputs:
- weights: float32 [65536, 64], P(('region', 'feat'), 'row')
- duals: float32 [65536, 64], P(('region', 'feat'), 'row')
- consensus: float32 [4096, 64], P('feat', 'row')
- penalty: float32 [16, 3], P('region')
Inputs may be any that keep to these rules, and one draw needn't show every extreme that they name: factors: each 1024 x 1024 block is lower triangular, its diagonal between 3.5 and 5, its entries below the diagonal drawn independently, symmetric about zero and at most 0.08 in magnitude.
All inputs are finite; a program needn't handle non-finite values. No bound on the sum of `member` on one device may be relied on, other than what follows from the above.
Results may differ from a plain program's by a relative error of at most 0.006.
Values may be sent and summed in bfloat16 or wider, within the bound.
A program may use at most 128 MiB of HBM per device.

v0:
```python
import math

import jax
import jax.numpy as jnp
from jax import lax
from jax.sharding import PartitionSpec as P

FEATURES = 4096
OUTPUTS = 64
ITERS = 3


def from_everyone(value, axis):
    size = lax.axis_size(axis)
    return lax.all_to_all(
        jnp.broadcast_to(value[None], (size, *value.shape)), axis, 0, 0, tiled=True
    )


def joined_along(blocks, dim):
    blocks = jnp.moveaxis(blocks, 0, dim)
    dims = blocks.shape
    return blocks.reshape(*dims[:dim], dims[dim] * dims[dim + 1], *dims[dim + 2 :])


def gathered_copies(value, axis, dim):
    blocks = from_everyone(value, axis)
    return joined_along(blocks, dim)


def in_blocks(value, dim, size):
    dims = value.shape
    blocks = value.reshape(*dims[:dim], size, dims[dim] // size, *dims[dim + 1 :])
    return jnp.moveaxis(blocks, dim, 0)


def summed_on_arrival(value, axis, dim):
    blocks = in_blocks(value, dim, lax.axis_size(axis))
    arrived = lax.all_to_all(blocks, axis, split_axis=0, concat_axis=0, tiled=True)
    return arrived.astype(jnp.float32).sum(axis=0)


def sent_and_summed(value, axis, dim):
    blocks = in_blocks(value, dim, lax.axis_size(axis))
    arrived = lax.all_to_all(blocks, axis, split_axis=0, concat_axis=0, tiled=True)
    return arrived.sum(axis=0)


def over_copies(value, axis):
    everything = from_everyone(value, axis)
    return jnp.sum(everything, axis=0)


def in_one(arrays, axis):
    ends = [0]
    for a in arrays:
        ends.append(ends[-1] + a.size)
    so_far = over_copies(jnp.concatenate([a.ravel() for a in arrays]), axis)
    return tuple((so_far[b:e].reshape(a.shape) for a, b, e in zip(arrays, ends, ends[1:])))


def block_solve(factor, right_side):
    forward = lax.linalg.triangular_solve(factor, right_side, left_side=True, lower=True)
    return lax.linalg.triangular_solve(
        factor, forward, left_side=True, lower=True, transpose_a=True
    )


def per_device(
    samples,
    targets,
    member,
    omega,
    phase,
    factors,
    weights_init,
    duals_init,
    consensus_init,
    penalty_init,
):
    angle = jnp.dot(samples, omega, preferred_element_type=jnp.float32) + phase
    features = (math.sqrt(2.0 / FEATURES) * jnp.cos(angle)).astype(jnp.bfloat16)
    offset = 0.01 * FEATURES * OUTPUTS
    weights, duals, consensus = (weights_init, duals_init, consensus_init)
    penalty = penalty_init
    history = []
    for iteration in range(ITERS):
        coarse = gathered_copies(weights.astype(jnp.bfloat16), "row", 1)
        partial_value = jnp.dot(features, coarse, preferred_element_type=jnp.float32)
        share = summed_on_arrival(partial_value.astype(jnp.bfloat16), "feat", 0)
        height = share.shape[0]
        first = lax.axis_index("feat") * height
        wanted = lax.dynamic_slice_in_dim(targets, first, height, 0).astype(jnp.float32)
        chosen = lax.dynamic_slice_in_dim(member, first, height, 0).astype(jnp.float32)
        piece = (chosen[:, None] * (share - wanted)).astype(jnp.bfloat16)
        residual = gathered_copies(piece, "feat", 0)
        gradient = lax.dot_general(
            features, residual, (((0,), (0,)), ((), ())), preferred_element_type=jnp.float32
        )
        gradient = sent_and_summed(gradient, "row", 1)
        scalar = penalty[0]
        right_side = gradient + scalar * (weights - consensus + duals)
        weights = weights - block_solve(factors, right_side)
        total, weight_sum = in_one((scalar * (weights + duals), penalty), "region")
        updated = total / weight_sum[0]
        duals = duals + weights - updated
        gap_part = jnp.sum(jnp.square(weights - updated))
        drift_part = jnp.sum(jnp.square(updated - consensus))
        gap, drift = in_one((gap_part, drift_part), ("feat", "row"))
        drift = scalar * scalar * drift
        renewed = penalty * jnp.sqrt((gap + offset) / (drift + offset))
        duals = duals * (scalar / renewed[0])
        consensus = updated
        penalty = renewed
        history.append(renewed)
    return (weights, duals, consensus, jnp.stack(history, axis=1))


def solution(mesh):
    return jax.shard_map(
        per_device,
        mesh=mesh,
        in_specs=(
            P(("region", "row"), None),
            P(("region", "row"), None),
            P(("region", "row")),
            P(None, "feat"),
            P("feat"),
            P(("region", "feat"), None),
            P(("region", "feat"), "row"),
            P(("region", "feat"), "row"),
            P("feat", "row"),
            P("region"),
        ),
        out_specs=(
            P(("region", "feat"), "row"),
            P(("region", "feat"), "row"),
            P("feat", "row"),
            P("region", None),
        ),
        check_vma=False,
    )
```

profile of v0, /device:TPU:1, one launch (start us, length us, event | category | flops | bytes accessed | tf_op | source)
XLA Modules:
  0.0 664.9 jit_solution(4227901309036374622)
XLA Ops:
  2.3 5.0 all-to-all-start
  7.3 115.6 %multiply_convert_fusion = bf16[8192,1024]{1,0:T(8,128)(2,1)} fusion(f32[1024]{0:T(1024)} %param.18, bf16[8192,128]{1,0:T(8,128)(2,1)S(1)} %copy-done, bf16[128,1024]{1,0:T(8,128)(2,1)} %param.17), kind=kOutput, calls=%fused_computation.2 | convolution fusion | flops 2172649472 | bytes 19140608 | tf_op jit(solution)/shard_map/dot_general | solution.py:81
  122.9 11.0 %convolution_convert_fusion.2 = bf16[8192,64]{0,1:T(8,128)(2,1)S(1)} fusion(bf16[8192,1024]{1,0:T(8,128)(2,1)} %multiply_convert_fusion, bf16[1024,64]{0,1:T(8,128)(2,1)S(1)} %bitcast.368), kind=kOutput, calls=%fused_computation.11 | convolution fusion | flops 1074266112 | bytes 17956864 | tf_op jit(solution)/shard_map/dot_general | solution.py:89
  135.0 5.1 all-to-all-start.1
  140.7 12.8 %all-to-all-done.1 = bf16[4,2048,64]{1,2,0:T(8,128)(2,1)S(1)} async-done(((bf16[4,2048,64]{1,2,0:T(8,128)(2,1)}), bf16[4,2048,64]{1,2,0:T(8,128)(2,1)S(1)}, u32[]{:S(2)}, u32[]{:S(2)}) %all-to-all-start.1) | async-done | bytes 1048608 | tf_op jit(solution)/shard_map/all_to_all | solution.py:39
  155.8 4.5 all-to-all-start.2
  160.3 4.7 fusion.6
  165.0 8.7 %all-to-all-done.2 = bf16[4,2048,64]{1,2,0:T(8,128)(2,1)S(1)} async-done(((bf16[4,2048,64]{1,2,0:T(8,128)(2,1)}), bf16[4,2048,64]{1,2,0:T(8,128)(2,1)S(1)}, u32[]{:S(2)}, u32[]{:S(2)}) %all-to-all-start.2) | async-done | bytes 1048608 | tf_op jit(solution)/shard_map/all_to_all | solution.py:15
  173.9 9.5 %fusion.7 = f32[4,1024,16]{1,2,0:T(8,128)} fusion(bf16[4,16,8192]{2,1,0:T(8,128)(2,1)S(1)} %bitcast.366, bf16[8192,1024]{1,0:T(8,128)(2,1)} %multiply_convert_fusion), kind=kOutput, calls=%fused_computation.17 | convolution fusion | flops 1073741824 | bytes 18087936 | tf_op jit(solution)/shard_map/dot_general | solution.py:97
  183.4 4.9 all-to-all-start.3
  188.3 28.1 %while.12 = (s32[]{:T(128)}, f32[1024,1024]{1,0:T(8,128)}, s32[8,2]{0,1:T(2,128)S(1)}, f32[8,128,128]{2,1,0:T(8,128)}, s32[]{:T(128)}) while((s32[]{:T(128)}, f32[1024,1024]{1,0:T(8,128)}, s32[8,2]{0,1:T(2,128)S(1)}, f32[8,128,128]{2,1,0:T(8,128)}, s32[]{:T(128)}) %tuple.125), condition=%wide.while_cond.1, body=%wide.while_body.1.sunk | while | flops 2 | bytes 132205 | solution.py:64
  188.9 2.9 bitcast_dynamic-update-slice_fusion.2
  192.5 2.9 bitcast_dynamic-update-slice_fusion.2
  196.0 2.9 bitcast_dynamic-update-slice_fusion.2
  199.5 2.9 bitcast_dynamic-update-slice_fusion.2
  203.0 2.9 bitcast_dynamic-update-slice_fusion.2
  206.5 2.9 bitcast_dynamic-update-slice_fusion.2
  210.1 2.9 bitcast_dynamic-update-slice_fusion.2
  213.6 2.8 bitcast_dynamic-update-slice_fusion.2
  217.1 79.4 %custom-call.11 = f32[8,128,128]{1,2,0:T(8,128)S(1)} custom-call(f32[8,128,128]{2,1,0:T(8,128)} %get-tuple-element.47), custom_call_target="InvertDiagBlocksLowerTriangular" | custom-call | tf_op jit(solution)/shard_map/triangular_solve/custom-call.0 | solution.py:64
  305.3 1.6 convolution_subtract_fusion.39
  318.5 39.4 %all_to_all.96 = f32[16,1,16385]{2,1,0:T(1,128)} all-to-all(f32[16,1,16385]{2,1,0:T(1,128)S(1)} %broadcast_in_dim.28), channel_id=1, replica_groups=mesh['region'=16,'feat'=4,'row'=4] {'region'}, dimensions={0} | all-to-all | bytes 2097280 | tf_op jit(solution)/shard_map/all_to_all | solution.py:15
  357.9 1.9 reduce_sum.166
  362.0 8.7 %all_to_all.97 = bf16[4,1024,16]{1,2,0:T(8,128)(2,1)S(1)} all-to-all(bf16[4,1024,16]{1,2,0:T(8,128)(2,1)S(1)} %broadcast_in_dim.26), channel_id=1, replica_groups=mesh['region'=16,'feat'=4,'row'=4] {'row'}, dimensions={0} | all-to-all | bytes 262144 | tf_op jit(solution)/shard_map/all_to_all | solution.py:15
  370.7 11.0 %convolution_convert_fusion.1 = bf16[8192,64]{0,1:T(8,128)(2,1)S(1)} fusion(bf16[8192,1024]{1,0:T(8,128)(2,1)} %multiply_convert_fusion, bf16[1024,64]{0,1:T(8,128)(2,1)S(1)} %bitcast.369), kind=kOutput, calls=%fused_computation.10 | convolution fusion | flops 1074266112 | bytes 17956864 | tf_op jit(solution)/shard_map/dot_general | solution.py:89
  381.7 20.3 %all_to_all.98 = bf16[4,2048,64]{1,2,0:T(8,128)(2,1)S(1)} all-to-all(bf16[4,2048,64]{1,2,0:T(8,128)(2,1)S(1)} %bitcast.363), channel_id=1, replica_groups=mesh['region'=16,'feat'=4,'row'=4] {'feat'}, dimensions={0} | all-to-all | bytes 2097152 | tf_op jit(solution)/shard_map/all_to_all | solution.py:39
  404.3 4.5 all-to-all-start.6
  411.1 11.2 %all-to-all-done.6 = bf16[4,2048,64]{1,2,0:T(8,128)(2,1)S(1)} async-done(((bf16[4,2048,64]{1,2,0:T(8,128)(2,1)}), bf16[4,2048,64]{1,2,0:T(8,128)(2,1)S(1)}, u32[]{:S(2)}, u32[]{:S(2)}) %all-to-all-start.6) | async-done | bytes 1048608 | tf_op jit(solution)/shard_map/all_to_all | solution.py:15
  422.9 4.3 all-to-all-start.9
  427.2 9.5 %fusion.10 = f32[4,1024,16]{1,2,0:T(8,128)} fusion(bf16[4,16,8192]{2,1,0:T(8,128)(2,1)S(1)} %bitcast.367, bf16[8192,1024]{1,0:T(8,128)(2,1)} %multiply_convert_fusion), kind=kOutput, calls=%fused_computation.18 | convolution fusion | flops 1073741824 | bytes 18087936 | tf_op jit(solution)/shard_map/dot_general | solution.py:97
  436.7 4.3 all-to-all-start.7
  443.1 3.8 all-to-all-done.7
  455.7 1.6 convolution_subtract_fusion.33
  468.9 32.2 %all_to_all.99 = f32[16,1,16385]{2,1,0:T(1,128)} all-to-all(f32[16,1,16385]{2,1,0:T(1,128)S(1)} %broadcast_in_dim.32), channel_id=1, replica_groups=mesh['region'=16,'feat'=4,'row'=4] {'region'}, dimensions={0} | all-to-all | bytes 2097280 | tf_op jit(solution)/shard_map/all_to_all | solution.py:15
  501.1 1.9 reduce_sum.172
  503.5 1.9 multiply_reduce_fusion.3
  506.4 7.2 %all_to_all.100 = bf16[4,1024,16]{1,2,0:T(8,128)(2,1)S(1)} all-to-all(bf16[4,1024,16]{1,2,0:T(8,128)(2,1)S(1)} %broadcast_in_dim.30), channel_id=1, replica_groups=mesh['region'=16,'feat'=4,'row'=4] {'row'}, dimensions={0} | all-to-all | bytes 262144 | tf_op jit(solution)/shard_map/all_to_all | solution.py:15
  513.6 11.0 %convolution_convert_fusion = bf16[8192,64]{0,1:T(8,128)(2,1)S(1)} fusion(bf16[8192,1024]{1,0:T(8,128)(2,1)} %multiply_convert_fusion, bf16[1024,64]{0,1:T(8,128)(2,1)S(1)} %bitcast.370), kind=kOutput, calls=%fused_computation.9 | convolution fusion | flops 1074266112 | bytes 17956864 | tf_op jit(solution)/shard_map/dot_general | solution.py:89
  524.7 20.2 %all_to_all.101 = bf16[4,2048,64]{1,2,0:T(8,128)(2,1)S(1)} all-to-all(bf16[4,2048,64]{1,2,0:T(8,128)(2,1)S(1)} %bitcast.364), channel_id=1, replica_groups=mesh['region'=16,'feat'=4,'row'=4] {'feat'}, dimensions={0} | all-to-all | bytes 2097152 | tf_op jit(solution)/shard_map/all_to_all | solution.py:39
  547.2 4.5 all-to-all-start.12
  553.1 12.1 %all-to-all-done.12 = bf16[4,2048,64]{1,2,0:T(8,128)(2,1)S(1)} async-done(((bf16[4,2048,64]{1,2,0:T(8,128)(2,1)}), bf16[4,2048,64]{1,2,0:T(8,128)(2,1)S(1)}, u32[]{:S(2)}, u32[]{:S(2)}) %all-to-all-start.12) | async-done | bytes 1048608 | tf_op jit(solution)/shard_map/all_to_all | solution.py:15
  565.8 4.6 all-to-all-start.15
  570.5 9.5 %fusion.13 = f32[4,1024,16]{1,2,0:T(8,128)} fusion(bf16[4,16,8192]{2,1,0:T(8,128)(2,1)S(1)} %bitcast.365, bf16[8192,1024]{1,0:T(8,128)(2,1)} %multiply_convert_fusion), kind=kOutput, calls=%fused_computation.19 | convolution fusion | flops 1073741824 | bytes 18087936 | tf_op jit(solution)/shard_map/dot_general | solution.py:97
  580.0 4.1 all-to-all-start.13
  586.2 3.8 all-to-all-done.13
  612.1 31.5 %all_to_all.102 = f32[16,1,16385]{2,1,0:T(1,128)S(1)} all-to-all(f32[16,1,16385]{2,1,0:T(1,128)S(1)} %broadcast_in_dim.34), channel_id=1, replica_groups=mesh['region'=16,'feat'=4,'row'=4] {'region'}, dimensions={0} | all-to-all | bytes 2097280 | tf_op jit(solution)/shard_map/all_to_all | solution.py:15
  649.0 6.7 %all-to-all-start.17 = ((f32[16,1,2]{2,1,0:T(1,128)}), f32[16,1,2]{2,1,0:T(1,128)S(1)}, u32[]{:S(2)}, u32[]{:S(2)}) async-start(f32[16,1,2]{2,1,0:T(1,128)} %broadcast_in_dim.35), calls=%async_computation.17 | async-start | bytes 16384 | tf_op jit(solution)/shard_map/all_to_all | solution.py:15
  655.7 5.4 all-to-all-done.17
  (263 shorter events, 94.9 us)
Async XLA Ops:
  0.6 6.7 %copy-start = (bf16[8192,128]{1,0:T(8,128)(2,1)S(1)}, bf16[8192,128]{1,0:T(8,128)(2,1)}, u32[]{:S(2)}) copy-start(bf16[8192,128]{1,0:T(8,128)(2,1)} %param.14) | copy-start | bytes 6291460
  2.3 120.6 %all-to-all-start = ((bf16[4,1024,16]{1,2,0:T(8,128)(2,1)}), bf16[4,1024,16]{1,2,0:T(8,128)(2,1)S(1)}, u32[]{:S(2)}, u32[]{:S(2)}) async-start(bf16[4,1024,16]{1,2,0:T(8,128)(2,1)} %broadcast_in_dim.24), calls=%async_computation | async-start | bytes 262144 | tf_op jit(solution)/shard_map/all_to_all | solution.py:15
  135.0 18.5 %all-to-all-start.1 = ((bf16[4,2048,64]{1,2,0:T(8,128)(2,1)}), bf16[4,2048,64]{1,2,0:T(8,128)(2,1)S(1)}, u32[]{:S(2)}, u32[]{:S(2)}) async-start(bf16[4,2048,64]{1,2,0:T(8,128)(2,1)} %bitcast.345), calls=%async_computation.1 | async-start | bytes 2097152 | tf_op jit(solution)/shard_map/all_to_all | solution.py:39
  155.8 17.9 %all-to-all-start.2 = ((bf16[4,2048,64]{1,2,0:T(8,128)(2,1)}), bf16[4,2048,64]{1,2,0:T(8,128)(2,1)S(1)}, u32[]{:S(2)}, u32[]{:S(2)}) async-start(bf16[4,2048,64]{1,2,0:T(8,128)(2,1)} %broadcast_in_dim.25), calls=%async_computation.2 | async-start | bytes 2097152 | tf_op jit(solution)/shard_map/all_to_all | solution.py:15
  173.8 122.7 %copy-start.3 = (f32[1024,16]{0,1:T(8,128)S(1)}, f32[1024,16]{0,1:T(8,128)}, u32[]{:S(2)}) copy-start(f32[1024,16]{0,1:T(8,128)} %param.20) | copy-start | bytes 196612
  173.8 122.7 %copy-start.4 = (f32[1024,16]{0,1:T(8,128)S(1)}, f32[1024,16]{0,1:T(8,128)}, u32[]{:S(2)}) copy-start(f32[1024,16]{0,1:T(8,128)} %param.22) | copy-start | bytes 196612
  173.9 122.7 %copy-start.6 = (f32[1024,16]{0,1:T(8,128)S(1)}, f32[1024,16]{0,1:T(8,128)}, u32[]{:S(2)}) copy-start(f32[1024,16]{0,1:T(8,128)} %param.21) | copy-start | bytes 196612
  183.4 113.1 %all-to-all-start.3 = ((f32[4,1024,16]{1,2,0:T(8,128)}), f32[4,1024,16]{1,2,0:T(8,128)S(1)}, u32[]{:S(2)}, u32[]{:S(2)}) async-start(f32[4,1024,16]{1,2,0:T(8,128)} %fusion.7), calls=%async_computation.3 | async-start | bytes 524288 | tf_op jit(solution)/shard_map/all_to_all | solution.py:45
  404.3 18.0 %all-to-all-start.6 = ((bf16[4,2048,64]{1,2,0:T(8,128)(2,1)}), bf16[4,2048,64]{1,2,0:T(8,128)(2,1)S(1)}, u32[]{:S(2)}, u32[]{:S(2)}) async-start(bf16[4,2048,64]{1,2,0:T(8,128)(2,1)} %broadcast_in_dim.27), calls=%async_computation.6 | async-start | bytes 2097152 | tf_op jit(solution)/shard_map/all_to_all | solution.py:15
  422.9 13.8 %all-to-all-start.9 = ((f32[16,1,2]{2,1,0:T(1,128)}), f32[16,1,2]{2,1,0:T(1,128)S(1)}, u32[]{:S(2)}, u32[]{:S(2)}) async-start(f32[16,1,2]{2,1,0:T(1,128)} %broadcast_in_dim.29), calls=%async_computation.9 | async-start | bytes 16384 | tf_op jit(solution)/shard_map/all_to_all | solution.py:15
  436.7 10.2 %all-to-all-start.7 = ((f32[4,1024,16]{1,2,0:T(8,128)}), f32[4,1024,16]{1,2,0:T(8,128)S(1)}, u32[]{:S(2)}, u32[]{:S(2)}) async-start(f32[4,1024,16]{1,2,0:T(8,128)} %fusion.10), calls=%async_computation.7 | async-start | bytes 524288 | tf_op jit(solution)/shard_map/all_to_all | solution.py:45
  547.2 18.0 %all-to-all-start.12 = ((bf16[4,2048,64]{1,2,0:T(8,128)(2,1)}), bf16[4,2048,64]{1,2,0:T(8,128)(2,1)S(1)}, u32[]{:S(2)}, u32[]{:S(2)}) async-start(bf16[4,2048,64]{1,2,0:T(8,128)(2,1)} %broadcast_in_dim.31), calls=%async_computation.12 | async-start | bytes 2097152 | tf_op jit(solution)/shard_map/all_to_all | solution.py:15
  565.8 14.2 %all-to-all-start.15 = ((f32[16,1,2]{2,1,0:T(1,128)}), f32[16,1,2]{2,1,0:T(1,128)S(1)}, u32[]{:S(2)}, u32[]{:S(2)}) async-start(f32[16,1,2]{2,1,0:T(1,128)} %broadcast_in_dim.33), calls=%async_computation.15 | async-start | bytes 16384 | tf_op jit(solution)/shard_map/all_to_all | solution.py:15
  580.0 10.0 %all-to-all-start.13 = ((f32[4,1024,16]{1,2,0:T(8,128)}), f32[4,1024,16]{1,2,0:T(8,128)S(1)}, u32[]{:S(2)}, u32[]{:S(2)}) async-start(f32[4,1024,16]{1,2,0:T(8,128)} %fusion.13), calls=%async_computation.13 | async-start | bytes 524288 | tf_op jit(solution)/shard_map/all_to_all | solution.py:45
  609.3 55.1 %copy-start.1 = (bf16[8192,128]{1,0:T(8,128)(2,1)S(1)}, bf16[8192,128]{1,0:T(8,128)(2,1)}, u32[]{:S(2)}) copy-start(bf16[8192,128]{1,0:T(8,128)(2,1)} %param.14) | copy-start | bytes 6291460
  611.2 53.2 %copy-start.5 = (f32[1024,16]{0,1:T(8,128)}, f32[1024,16]{0,1:T(8,128)S(1)}, u32[]{:S(2)}) copy-start(f32[1024,16]{0,1:T(8,128)S(1)} %get-tuple-element.84) | copy-start | bytes 196612
  646.4 18.0 %copy-start.2 = (f32[1024,16]{0,1:T(8,128)}, f32[1024,16]{0,1:T(8,128)S(1)}, u32[]{:S(2)}) copy-start(f32[1024,16]{0,1:T(8,128)S(1)} %copy.95) | copy-start | bytes 196612
  649.0 12.1 %all-to-all-start.17 = ((f32[16,1,2]{2,1,0:T(1,128)}), f32[16,1,2]{2,1,0:T(1,128)S(1)}, u32[]{:S(2)}, u32[]{:S(2)}) async-start(f32[16,1,2]{2,1,0:T(1,128)} %broadcast_in_dim.35), calls=%async_computation.17 | async-start | bytes 16384 | tf_op jit(solution)/shard_map/all_to_all | solution.py:15
where the time goes:
time: 676 us; the launch traced here: 665 us
  matrix products  239 us (35%)
  blocking collectives  159 us (24%)
  other arithmetic  106 us (16%)
  waiting for transfers between devices  57.7 us (9%)
  starting transfers between devices  52.5 us (8%)
  local copies, waits for them, and re-layouts  43.4 us (6%)
  between operations  7.03 us (1%)
    all_to_all x5, blocking collectives, from_everyone(): lax.all_to_all(jnp.broadcast_to(value[None], (size, *value.shape)), axis,...  119 us
    dot_general x1, matrix products, per_device(): angle = jnp.dot(samples, omega, preferred_element_type=jnp.float32) + phase  116 us
    another operation x4, other arithmetic, block_solve(): lax.linalg.triangular_solve(factor, forward, left_side=True, lower=True,...  84.1 us
    all_to_all x2, blocking collectives, summed_on_arrival(): lax.all_to_all(blocks, axis, split_axis=0, concat_axis=0, tiled=True)  40.5 us
    all_to_all x7, waiting for transfers between devices, from_everyone(): lax.all_to_all(jnp.broadcast_to(value[None], (size, *value.shape)), axis,...  37.4 us
    all_to_all x7, starting transfers between devices, from_everyone(): lax.all_to_all(jnp.broadcast_to(value[None], (size, *value.shape)), axis,...  34 us
    dot_general x3, matrix products, per_device(): jnp.dot(features, coarse, preferred_element_type=jnp.float32)  32.9 us
    another operation x45, matrix products, block_solve(): lax.linalg.triangular_solve(factor, right_side, left_side=True, lower=True)  31.4 us
  transfers between devices with their start and end apart: 11, of which 7 were waited for; matrix products, arithmetic and copies ran while one was open for 38% of the time, Pallas kernels for 0%

commit v1 on v0

v1 whole, which is shorter than its diff:
```python
import math

import jax
import jax.numpy as jnp
from jax import lax
from jax.experimental import pallas as pl
from jax.experimental.pallas import tpu as pltpu
from jax.sharding import PartitionSpec as P

FEATURES = 4096
OUTPUTS = 64
ITERS = 3
REGIONS = 16
ROWS = 4
FEATS = 4
BLOCK = 1024
INPUTS = 128
CHIP = 4096
HALF = 2048
SLICE = 16
MESH = pl.DeviceIdType.MESH
F32 = jnp.float32
BF16 = jnp.bfloat16
SINE = (6.2831640442521435, -41.33714236464144, 81.34076868066526, -70.99343137755689)
NT = (((1,), (1,)), ((), ()))


def dot(a, b):
    return jnp.dot(a, b, preferred_element_type=F32)


def dot_nt(a, b):
    return lax.dot_general(a, b, NT, preferred_element_type=F32)


def remote(src, dst, send, recv, device):
    return pltpu.make_async_remote_copy(
        src_ref=src,
        dst_ref=dst,
        send_sem=send,
        recv_sem=recv,
        device_id=device,
        device_id_type=MESH,
    )


def kernel(
    samples,
    targets,
    member,
    omega,
    phase,
    factors,
    w_in,
    u_in,
    z_in,
    rho_in,
    w_out,
    u_out,
    z_out,
    pen_out,
    feat,
    twice,
    omegas,
    phases,
    rhs,
    tgt,
    mem,
    low,
    inv,
    weights,
    own,
    pred_send,
    pred_recv,
    res_own,
    res_other,
    acc,
    grad_send,
    grad_recv,
    cons_src,
    cons_sum,
    cons_all,
    gaps,
    w,
    u,
    z,
    local,
    om_s,
    om_r,
    ag_s,
    ag_r,
    rs_s,
    rs_r,
    pair_s,
    pair_r,
    cs_s,
    cs_r,
    ca_s,
    ca_r,
    gp_s,
    gp_r,
):
    reg = lax.axis_index("region")
    f = lax.axis_index("feat")
    y = lax.axis_index("row")
    core = lax.rem(f, 2)
    xl = f // 2
    xh = lax.rem(reg, 2)
    partner = (reg, xl * 2 + 1 - core, y)

    def chip(k):
        dx, dy = divmod(k, ROWS)
        return lax.rem(xl + dx, 2), lax.rem(y + dy, ROWS)

    def chip_device(k):
        tx, ty = chip(k)
        return (reg, tx * 2 + core, ty)

    def group_device(k):
        df, dy = divmod(k, ROWS)
        return (reg, lax.rem(f + df, FEATS), lax.rem(y + dy, ROWS))

    def region_device(k):
        return (lax.rem(reg + k, REGIONS), f, y)

    across = (reg, (1 - xl) * 2 + core, y)
    beside = (reg - xh + 1 - xh, (1 - xl) * 2 + core, y)

    mine = pl.ds(pl.multiple_of(xl * CHIP, CHIP), CHIP)
    half = xl * CHIP + core * HALF
    loads = [
        pltpu.make_async_copy(omega, omegas.at[xl], local.at[0]),
        pltpu.make_async_copy(phase, phases.at[xl], local.at[1]),
        pltpu.make_async_copy(samples.at[mine, :], twice.at[:, pl.ds(0, INPUTS)], local.at[2]),
        pltpu.make_async_copy(
            samples.at[mine, :], twice.at[:, pl.ds(INPUTS, INPUTS)], local.at[3]
        ),
        pltpu.make_async_copy(
            targets.at[:, pl.ds(pl.multiple_of(half, HALF), HALF)], tgt, local.at[4]
        ),
        pltpu.make_async_copy(
            member.at[pl.ds(pl.multiple_of(half // 128, 16), 16), :], mem, local.at[5]
        ),
        pltpu.make_async_copy(factors, low, local.at[6]),
    ]
    for load in loads:
        load.start()

    barrier = pltpu.get_barrier_semaphore()
    for k in range(1, FEATS * ROWS):
        pl.semaphore_signal(barrier, inc=1, device_id=group_device(k), device_id_type=MESH)
    for k in range(1, REGIONS):
        pl.semaphore_signal(barrier, inc=1, device_id=region_device(k), device_id_type=MESH)
    pl.semaphore_signal(barrier, inc=1, device_id=beside, device_id_type=MESH)

    w[...] = w_in[...]
    u[...] = u_in[...]
    z[...] = z_in[...]
    weights[0, xl, y] = w_in[...].astype(BF16)

    for load in loads[:4]:
        load.wait()

    scale = math.sqrt(2.0 / FEATURES)
    c1, c3, c5, c7 = (-scale * c for c in SINE)

    def make_features(j):
        turns = omegas[j].astype(F32) * (0.5 / math.pi)
        high = turns.astype(BF16)
        rhs[pl.ds(0, INPUTS), :] = high
        rhs[pl.ds(INPUTS, INPUTS), :] = (turns - high.astype(F32)).astype(BF16)
        shift = phases[j] * (0.5 / math.pi)

        def body(i, _):
            for m in range(2):
                rows = pl.ds(pl.multiple_of(i * 512 + m * 256, 256), 256)
                lhs = twice[rows, :]
                for n in range(4):
                    cols = pl.ds(n * 256, 256)
                    turn = dot(lhs, rhs[:, cols]) + shift[:, n * 256 : n * 256 + 256]
                    g = jnp.abs(turn - jnp.round(turn)) - 0.25
                    s = g * g
                    feat[j, rows, cols] = (g * (c1 + s * (c3 + s * (c5 + s * c7)))).astype(BF16)
            return 0

        lax.fori_loop(0, CHIP // 512, body, 0)

    make_features(xl)

    pl.semaphore_wait(barrier, 31)

    om = [
        remote(
            omegas.at[xl, pl.ds(0, 64), :],
            omegas.at[xl, pl.ds(0, 64), :],
            om_s.at[0],
            om_r.at[0],
            across,
        ),
        remote(
            omegas.at[xl, pl.ds(64, 64), :],
            omegas.at[xl, pl.ds(64, 64), :],
            om_s.at[1],
            om_r.at[1],
            beside,
        ),
        remote(phases.at[xl], phases.at[xl], om_s.at[2], om_r.at[2], across),
    ]
    om_in = [
        remote(
            omegas.at[1 - xl, pl.ds(0, 64), :],
            omegas.at[1 - xl, pl.ds(0, 64), :],
            om_s.at[0],
            om_r.at[0],
            across,
        ),
        remote(
            omegas.at[1 - xl, pl.ds(64, 64), :],
            omegas.at[1 - xl, pl.ds(64, 64), :],
            om_s.at[1],
            om_r.at[1],
            beside,
        ),
        remote(phases.at[1 - xl], phases.at[1 - xl], om_s.at[2], om_r.at[2], across),
    ]
    for copy in om:
        copy.start()

    def gather(it):
        return [
            remote(
                weights.at[it, xl, y],
                weights.at[it, xl, y],
                ag_s.at[it, k],
                ag_r.at[it, k],
                chip_device(k),
            )
            for k in range(1, 8)
        ]

    def gather_in(it):
        out = []
        for k in range(1, 8):
            dx, dy = divmod(k, ROWS)
            sx, sy = lax.rem(xl + dx, 2), lax.rem(y + ROWS - dy, ROWS)
            out.append(
                remote(
                    weights.at[it, sx, sy],
                    weights.at[it, sx, sy],
                    ag_s.at[it, k],
                    ag_r.at[it, k],
                    chip_device(k),
                )
            )
        return out

    sent = list(om)

    def start(copies):
        for copy in copies:
            copy.start()
        sent.extend(copies)

    start_gather = gather(0)
    start(start_gather)

    for copy in om_in:
        copy.wait_recv()
    make_features(1 - xl)

    eye = lax.broadcasted_iota(jnp.int32, (128, 128), 0) == lax.broadcasted_iota(
        jnp.int32, (128, 128), 1
    )

    def make_inverse():
        ys, qs, columns, lanes = [], [], [], []
        inv[...] = jnp.zeros_like(inv)
        for b in range(8):
            at = pl.ds(b * 128, 128)
            block = low[at, at]
            diagonal = jnp.where(eye, block, 0.0)
            column = 1.0 / jnp.sum(diagonal, axis=1, keepdims=True)
            lanes.append(1.0 / jnp.sum(diagonal, axis=0, keepdims=True))
            columns.append(column)
            n = jnp.where(eye, 0.0, block) * column
            ys.append(-n)
            qs.append(dot(n.astype(BF16), n.astype(BF16)))
        for step in range(6):
            for b in range(8):
                q = qs[b].astype(BF16)
                if step < 5:
                    both = dot(jnp.concatenate([ys[b].astype(BF16), q], axis=0), q)
                    ys[b] = ys[b] + qs[b] + both[:128]
                    qs[b] = both[128:]
                else:
                    ys[b] = ys[b] + qs[b] + dot(ys[b].astype(BF16), q)
        for b in range(8):
            at = pl.ds(b * 128, 128)
            inv[at, at] = ys[b].astype(BF16)
        size = 128
        while size < BLOCK:
            for top in range(0, BLOCK, 2 * size):
                a = pl.ds(top, size)
                b = pl.ds(top + size, size)
                column = jnp.concatenate(
                    columns[(top + size) // 128 : (top + 2 * size) // 128], axis=0
                )
                c = low[b, a] * column
                t = c + dot(inv[b, b], c.astype(BF16))
                t = t + dot(t.astype(BF16), inv[a, a])
                inv[b, a] = (-t).astype(BF16)
            size *= 2
        return jnp.concatenate(lanes, axis=1)

    def predict(it, first):
        def body(i, _):
            for m in range(2):
                at = pl.multiple_of(i * 512 + m * 256, 256)
                rows = pl.ds(pl.multiple_of(first + at, 256), 256)
                both = dot_nt(weights[it, 0].reshape(OUTPUTS, BLOCK), feat[0, rows, :])
                both += dot_nt(weights[it, 1].reshape(OUTPUTS, BLOCK), feat[1, rows, :])
                own[:, pl.ds(at, 256)] = both
            return 0

        lax.fori_loop(0, HALF // 512, body, 0)

    def scale_to(value, shape):
        return jnp.broadcast_to(value, shape)

    def consensus_send(it, rho):
        value = scale_to(rho, (SLICE, BLOCK)) * (w[...] + u[...])
        for k in range(REGIONS):
            r, c = divmod(k, 8)
            cons_src[it, k, 0] = value[r * 8 : r * 8 + 8, c * 128 : c * 128 + 128]
            cons_src[it, k, 1] = scale_to(rho, (8, 128))
        cons_sum[it, reg] = cons_src[it, reg]
        start(
            [
                remote(
                    cons_src.at[it, lax.rem(reg + k, REGIONS)],
                    cons_sum.at[it, reg],
                    cs_s.at[it, k],
                    cs_r.at[it, k],
                    region_device(k),
                )
                for k in range(1, REGIONS)
            ]
        )

    def consensus_sum(it):
        for k in range(1, REGIONS):
            came = lax.rem(reg + REGIONS - k, REGIONS)
            remote(
                cons_src.at[it, came],
                cons_sum.at[it, came],
                cs_s.at[it, k],
                cs_r.at[it, k],
                region_device(k),
            ).wait_recv()
        total = cons_sum[it, 0]
        for k in range(1, REGIONS):
            total = total + cons_sum[it, k]
        cons_all[it, reg] = total[0] / total[1]
        start(
            [
                remote(
                    cons_all.at[it, reg],
                    cons_all.at[it, reg],
                    ca_s.at[it, k],
                    ca_r.at[it, k],
                    region_device(k),
                )
                for k in range(1, REGIONS)
            ]
        )

    def consensus_take(it):
        for k in range(1, REGIONS):
            came = lax.rem(reg + REGIONS - k, REGIONS)
            remote(
                cons_all.at[it, came],
                cons_all.at[it, came],
                ca_s.at[it, k],
                ca_r.at[it, k],
                region_device(k),
            ).wait_recv()
        gap = jnp.zeros((8, 128), F32)
        drift = jnp.zeros((8, 128), F32)
        for k in range(REGIONS):
            r, c = divmod(k, 8)
            at = (pl.ds(r * 8, 8), pl.ds(c * 128, 128))
            new = cons_all[it, k]
            apart = w[at] - new
            moved = new - z[at]
            gap += apart * apart
            drift += moved * moved
            u[at] = u[at] + apart
            z[at] = new
        row = lax.broadcasted_iota(jnp.int32, (8, 128), 0)
        gap = scale_to(jnp.sum(gap, axis=0, keepdims=True), (8, 128))
        drift = scale_to(jnp.sum(drift, axis=0, keepdims=True), (8, 128))
        me = f * ROWS + y
        gaps[it, me] = jnp.where(row == 0, gap, jnp.where(row == 1, drift, 0.0))
        start(
            [
                remote(
                    gaps.at[it, me], gaps.at[it, me], gp_s.at[it, k], gp_r.at[it, k], group_device(k)
                )
                for k in range(1, FEATS * ROWS)
            ]
        )

    def penalty(it, rho):
        for k in range(1, FEATS * ROWS):
            df, dy = divmod(k, ROWS)
            came = lax.rem(f + FEATS - df, FEATS) * ROWS + lax.rem(y + ROWS - dy, ROWS)
            remote(
                gaps.at[it, came], gaps.at[it, came], gp_s.at[it, k], gp_r.at[it, k], group_device(k)
            ).wait_recv()
        total = gaps[it, 0]
        for k in range(1, FEATS * ROWS):
            total = total + gaps[it, k]
        total = jnp.sum(total, axis=1, keepdims=True)
        offset = 0.01 * FEATURES * OUTPUTS
        gap, drift = total[0:1], rho * rho * total[1:2]
        new = rho * jnp.sqrt((gap + offset) / (drift + offset))
        u[...] = u[...] * scale_to(rho / new, (SLICE, BLOCK))
        pen_out[:, it : it + 1] = new
        return new

    for load in loads[4:]:
        load.wait()

    rho = jnp.full((1, 1), rho_in[0], F32)
    lanes = None
    mine_at = pl.multiple_of(core * HALF, HALF)
    other_at = pl.multiple_of((1 - core) * HALF, HALF)
    for it in range(ITERS):
        for copy in gather_in(it):
            copy.wait_recv()
        predict(it, other_at)
        pred_send[it] = own[...].astype(BF16)
        pred = remote(pred_send.at[it], pred_recv.at[it], pair_s.at[it, 0], pair_r.at[it, 0], partner)
        start([pred])
        predict(it, mine_at)
        if it:
            consensus_sum(it - 1)
        pred.wait_recv()
        for g in range(HALF // 128):
            at = pl.ds(g * 128, 128)
            value = own[:, at] + pred_recv[it, :, at].astype(F32) - tgt[:, at].astype(F32)
            res_own[it, :, at] = (mem[g : g + 1, :].astype(F32) * value).astype(BF16)
        res = remote(res_own.at[it], res_other.at[it], pair_s.at[it, 1], pair_r.at[it, 1], partner)
        start([res])

        def first_half(j, _):
            for n in range(4):
                cols = pl.ds(n * 256, 256)
                acc[j, :, cols] = dot(res_own[it], feat[j, pl.ds(mine_at, HALF), cols])
            return 0

        lax.fori_loop(0, 2, first_half, 0)
        res.wait_recv()
        for side in (1, 0):
            j = lax.rem(xl + side, 2)

            def second_half(n, _):
                cols = pl.ds(pl.multiple_of(n * 256, 256), 256)
                total = acc[j, :, cols] + dot(res_other[it], feat[j, pl.ds(other_at, HALF), cols])
                grad_send[it, j, :, :, cols] = total.reshape(ROWS, SLICE, 256).astype(BF16)
                return 0

            for n in range(4):
                second_half(n, 0)
            start(
                [
                    remote(
                        grad_send.at[it, chip(k)[0], chip(k)[1]],
                        grad_recv.at[it, k],
                        rs_s.at[it, k],
                        rs_r.at[it, k],
                        chip_device(k),
                    )
                    for k in range(side * 4, side * 4 + 4)
                    if k
                ]
            )
        if it == 0:
            lanes = make_inverse()
        else:
            consensus_take(it - 1)
            rho = penalty(it - 1, rho)
        gradient = grad_send[it, xl, y].astype(F32)
        for k in range(1, 8):
            remote(
                grad_send.at[it, 0, 0], grad_recv.at[it, k], rs_s.at[it, k], rs_r.at[it, k], across
            ).wait_recv()
        for k in range(1, 8):
            gradient = gradient + grad_recv[it, k].astype(F32)
        right = gradient + scale_to(rho, (SLICE, BLOCK)) * (w[...] - z[...] + u[...])
        right = right * lanes
        right = right + dot_nt(right.astype(BF16), inv[...])
        right = right + dot(right.astype(BF16), inv[...])
        new = w[...] - right * lanes
        w[...] = new
        if it < ITERS - 1:
            weights[it + 1, xl, y] = new.astype(BF16)
            start(gather(it + 1))
        consensus_send(it, rho)

    w_out[...] = w[...]
    consensus_sum(ITERS - 1)
    consensus_take(ITERS - 1)
    penalty(ITERS - 1, rho)
    u_out[...] = u[...]
    z_out[...] = z[...]
    for copy in sent:
        copy.wait_send()


def per_device(
    samples,
    targets,
    member,
    omega,
    phase,
    factors,
    weights_init,
    duals_init,
    consensus_init,
    penalty_init,
):
    hbm = pl.BlockSpec(memory_space=pl.ANY)
    vmem = pl.BlockSpec(memory_space=pltpu.VMEM)
    smem = pl.BlockSpec(memory_space=pltpu.SMEM)
    state = jax.ShapeDtypeStruct((SLICE, BLOCK), F32)
    dma = pltpu.SemaphoreType.DMA
    w, u, z, pen = pl.pallas_call(
        kernel,
        out_shape=(state, state, state, jax.ShapeDtypeStruct((1, ITERS), F32)),
        in_specs=[hbm] * 6 + [vmem] * 3 + [smem],
        out_specs=(vmem,) * 4,
        scratch_shapes=[
            pltpu.VMEM((2, CHIP, BLOCK), BF16),
            pltpu.VMEM((CHIP, 2 * INPUTS), BF16),
            pltpu.VMEM((2, INPUTS, BLOCK), BF16),
            pltpu.VMEM((2, 1, BLOCK), F32),
            pltpu.VMEM((2 * INPUTS, BLOCK), BF16),
            pltpu.VMEM((OUTPUTS, HALF), BF16),
            pltpu.VMEM((16, 128), jnp.int32),
            pltpu.VMEM((BLOCK, BLOCK), F32),
            pltpu.VMEM((BLOCK, BLOCK), BF16),
            pltpu.VMEM((ITERS, 2, ROWS, SLICE, BLOCK), BF16),
            pltpu.VMEM((OUTPUTS, HALF), F32),
            pltpu.VMEM((ITERS, OUTPUTS, HALF), BF16),
            pltpu.VMEM((ITERS, OUTPUTS, HALF), BF16),
            pltpu.VMEM((ITERS, OUTPUTS, HALF), BF16),
            pltpu.VMEM((ITERS, OUTPUTS, HALF), BF16),
            pltpu.VMEM((2, OUTPUTS, BLOCK), F32),
            pltpu.VMEM((ITERS, 2, ROWS, SLICE, BLOCK), BF16),
            pltpu.VMEM((ITERS, 8, SLICE, BLOCK), BF16),
            pltpu.VMEM((ITERS, REGIONS, 2, 8, 128), F32),
            pltpu.VMEM((ITERS, REGIONS, 2, 8, 128), F32),
            pltpu.VMEM((ITERS, REGIONS, 8, 128), F32),
            pltpu.VMEM((ITERS, FEATS * ROWS, 8, 128), F32),
            pltpu.VMEM((SLICE, BLOCK), F32),
            pltpu.VMEM((SLICE, BLOCK), F32),
            pltpu.VMEM((SLICE, BLOCK), F32),
            dma((7,)),
            dma((3,)),
            dma((3,)),
            dma((ITERS, 8)),
            dma((ITERS, 8)),
            dma((ITERS, 8)),
            dma((ITERS, 8)),
            dma((ITERS, 2)),
            dma((ITERS, 2)),
            dma((ITERS, REGIONS)),
            dma((ITERS, REGIONS)),
            dma((ITERS, REGIONS)),
            dma((ITERS, REGIONS)),
            dma((ITERS, REGIONS)),
            dma((ITERS, REGIONS)),
        ],
        compiler_params=pltpu.CompilerParams(
            collective_id=0, has_side_effects=True, vmem_limit_bytes=60 * 1024 * 1024
        ),
        name="admm",
    )(
        samples,
        targets.T,
        member.reshape(64, 128),
        omega,
        phase.reshape(1, BLOCK),
        factors,
        weights_init.T,
        duals_init.T,
        consensus_init.T,
        penalty_init,
    )
    return w.T, u.T, z.T, pen


def solution(mesh):
    return jax.shard_map(
        per_device,
        mesh=mesh,
        in_specs=(
            P(("region", "row"), None),
            P(("region", "row"), None),
            P(("region", "row")),
            P(None, "feat"),
            P("feat"),
            P(("region", "feat"), None),
            P(("region", "feat"), "row"),
            P(("region", "feat"), "row"),
            P("feat", "row"),
            P("region"),
        ),
        out_specs=(
            P(("region", "feat"), "row"),
            P(("region", "feat"), "row"),
            P("feat", "row"),
            P("region", None),
        ),
        check_vma=False,
    )
```

time: 676 us -> 127 us (0.19); the launches traced: 665 us -> 127 us
  matrix products: 239 us -> 0 us
  blocking collectives: 159 us -> 0 us
  Pallas kernels: 0 us -> 120 us
  other arithmetic: 106 us -> 0 us
  waiting for transfers between devices: 57.7 us -> 0 us
  starting transfers between devices: 52.5 us -> 0 us
  local copies, waits for them, and re-layouts: 43.4 us -> 5.55 us
    dot_general x7 -> x0, matrix products: 177 us -> none  [the longest x1 116 us: per_device(): angle = jnp.dot(samples, omega, preferred_element_type=jnp.float32) + phase]
    all_to_all x7 -> x0, blocking collectives: 159 us -> none  [the longest x5 119 us: from_everyone(): lax.all_to_all(jnp.broadcast_to(value[None], (size, *value.shape)), axis,...]
    pallas_call x0 -> x1, Pallas kernels: none -> 120 us  [per_device(): pl.pallas_call(kernel, out_shape=(state, state, state, jax.ShapeDtypeStru...]
    another operation x5 -> x0, other arithmetic: 84.7 us -> none  [the longest x4 84.1 us: block_solve(): lax.linalg.triangular_solve(factor, forward, left_side=True, lower=True,...]
    another operation x90 -> x0, matrix products: 61.8 us -> none  [the longest x45 31.4 us: block_solve(): lax.linalg.triangular_solve(factor, right_side, left_side=True, lower=True)]
    all_to_all x11 -> x0, waiting for transfers between devices: 57.7 us -> none  [the longest x7 37.4 us: from_everyone(): lax.all_to_all(jnp.broadcast_to(value[None], (size, *value.shape)), axis,...]
    all_to_all x11 -> x0, starting transfers between devices: 52.5 us -> none  [the longest x7 34 us: from_everyone(): lax.all_to_all(jnp.broadcast_to(value[None], (size, *value.shape)), axis,...]
    another operation x37 -> x0, local copies, waits for them, and re-layouts: 28.1 us -> none  [block_solve(): lax.linalg.triangular_solve(factor, forward, left_side=True, lower=True,...]
  transfers between devices with their start and end apart: 11 -> 0, of which waited for: 7 -> 0; matrix products, arithmetic and copies ran while one was open for 38% -> 0% of each run, Pallas kernels for 0% -> 0%
where the time goes in v1:
time: 127 us
  Pallas kernels  120 us (94%)
  local copies, waits for them, and re-layouts  5.55 us (4%)
  between operations  1.29 us (1%)
    pallas_call x1, Pallas kernels, per_device(): pl.pallas_call(kernel, out_shape=(state, state, state, jax.ShapeDtypeStru...  120 us
    unnamed x4, local copies, waits for them, and re-layouts  5.55 us

profile of v1, /device:TPU:1, one launch (start us, length us, event | category | flops | bytes accessed | tf_op | source)
XLA Modules:
  0.0 126.7 jit_solution(6002174334006874950)
XLA Ops:
  1.3 119.8 %admm.1 = (f32[16,1024]{1,0:T(8,128)}, f32[16,1024]{1,0:T(8,128)}, f32[16,1024]{1,0:T(8,128)}, f32[1,3]{1,0:T(1,128)}) custom-call(bf16[8192,128]{1,0:T(8,128)(2,1)} %samples.1, bf16[64,8192]{1,0:T(8,128)(2,1)} %bitcast.9, s32[64,128]{1,0:T(8,128)} %bitcast.16, bf16[128,1024]{1,0:T(8,128)(2,1)} %omega.1, f32[1,1024]{1,0:T(1,128)} %bitcast.17, ...), custom_call_target="tpu_custom_call" | custom-call | tf_op jit(solution)/shard_map/admm/pallas_call | solution.py:538
  121.1 1.5 %copy.19 = f32[1024,16]{0,1:T(8,128)} copy(f32[1024,16]{0,1:T(8,128)} %bitcast.15) | data formatting | bytes 131072
  122.6 1.5 %copy.20 = f32[1024,16]{0,1:T(8,128)} copy(f32[1024,16]{0,1:T(8,128)} %bitcast.14) | data formatting | bytes 131072
  124.1 1.5 %copy.21 = f32[1024,16]{0,1:T(8,128)} copy(f32[1024,16]{0,1:T(8,128)} %bitcast.13) | data formatting | bytes 131072
  125.6 1.1 copy.22

commit v2 on v1

v2 whole, which is shorter than its diff:
```python
import math

import jax
import jax.numpy as jnp
from jax import lax
from jax.experimental import pallas as pl
from jax.experimental.pallas import tpu as pltpu
from jax.sharding import PartitionSpec as P

FEATURES = 4096
OUTPUTS = 64
ITERS = 3
REGIONS = 16
ROWS = 4
FEATS = 4
BLOCK = 1024
INPUTS = 128
CHIP = 4096
HALF = 2048
SLICE = 16
MESH = pl.DeviceIdType.MESH
F32 = jnp.float32
BF16 = jnp.bfloat16
SINE = (6.2831640442521435, -41.33714236464144, 81.34076868066526, -70.99343137755689)
NT = (((1,), (1,)), ((), ()))
scope = jax.named_scope


def dot(a, b):
    return jnp.dot(a, b, preferred_element_type=F32)


def dot_nt(a, b):
    return lax.dot_general(a, b, NT, preferred_element_type=F32)


def remote(src, dst, send, recv, device):
    return pltpu.make_async_remote_copy(
        src_ref=src,
        dst_ref=dst,
        send_sem=send,
        recv_sem=recv,
        device_id=device,
        device_id_type=MESH,
    )


def kernel(
    samples,
    targets,
    member,
    omega,
    phase,
    factors,
    w_in,
    u_in,
    z_in,
    rho_in,
    w,
    u,
    z,
    pen_out,
    feat_mine,
    feat_other,
    sample,
    omegas,
    phases,
    rhs,
    turns_next,
    tgt,
    mem,
    low,
    inv,
    weights,
    pred,
    pred_send,
    pred_recv,
    res_own,
    res_other,
    acc,
    grad_send,
    grad_recv,
    cons_src,
    cons_sum,
    cons_all,
    rhos,
    gaps,
    local,
    om_s,
    om_r,
    ag_s,
    ag_r,
    rs_s,
    rs_r,
    pair_s,
    pair_r,
    cs_s,
    cs_r,
    ca_s,
    ca_r,
    gp_s,
    gp_r,
    ro_s,
    ro_r,
):
    reg = lax.axis_index("region")
    f = lax.axis_index("feat")
    y = lax.axis_index("row")
    core = lax.rem(f, 2)
    xl = f // 2
    xh = lax.rem(reg, 2)
    partner = (reg, xl * 2 + 1 - core, y)

    def chip(k):
        dx, dy = divmod(k, ROWS)
        return lax.rem(xl + dx, 2), lax.rem(y + dy, ROWS)

    def chip_device(k):
        tx, ty = chip(k)
        return (reg, tx * 2 + core, ty)

    def group_device(k):
        df, dy = divmod(k, ROWS)
        return (reg, lax.rem(f + df, FEATS), lax.rem(y + dy, ROWS))

    def region_device(k):
        return (lax.rem(reg + k, REGIONS), f, y)

    across = (reg, (1 - xl) * 2 + core, y)
    beside = (reg - xh + 1 - xh, (1 - xl) * 2 + core, y)

    first = xl * CHIP
    half = xl * CHIP + core * HALF
    early = 1024

    def rows_of(start, size):
        return pl.ds(pl.multiple_of(start, 128), size)

    loads = [
        pltpu.make_async_copy(omega, omegas.at[0], local.at[0]),
        pltpu.make_async_copy(phase, phases.at[0], local.at[1]),
        pltpu.make_async_copy(
            samples.at[rows_of(first, early), :], sample.at[pl.ds(0, early), :], local.at[2]
        ),
        pltpu.make_async_copy(w_in, w, local.at[3]),
        pltpu.make_async_copy(
            samples.at[rows_of(first + early, CHIP - early), :],
            sample.at[pl.ds(early, CHIP - early), :],
            local.at[4],
        ),
        pltpu.make_async_copy(u_in, u, local.at[5]),
        pltpu.make_async_copy(z_in, z, local.at[6]),
        pltpu.make_async_copy(targets.at[:, rows_of(half, HALF)], tgt, local.at[7]),
        pltpu.make_async_copy(
            member.at[pl.ds(pl.multiple_of(half // 128, 16), 16), :], mem, local.at[8]
        ),
        pltpu.make_async_copy(factors, low, local.at[9]),
    ]
    for load in loads:
        load.start()

    barrier = pltpu.get_barrier_semaphore()
    for k in range(1, FEATS * ROWS):
        pl.semaphore_signal(barrier, inc=1, device_id=group_device(k), device_id_type=MESH)
    for k in range(1, REGIONS):
        pl.semaphore_signal(barrier, inc=1, device_id=region_device(k), device_id_type=MESH)
    pl.semaphore_signal(barrier, inc=1, device_id=beside, device_id_type=MESH)

    with scope("load"):
        for load in loads[:3]:
            load.wait()

    scale = math.sqrt(2.0 / FEATURES)
    c1, c3, c5, c7 = (-scale * c for c in SINE)

    def make_rhs(side):
        turns = omegas[side].astype(F32) * (0.5 / math.pi)
        high = turns.astype(BF16)
        rest = (turns - high.astype(F32)).astype(BF16)
        for n in range(8):
            rhs[n, pl.ds(0, INPUTS), :] = high[:, n * 128 : n * 128 + 128]
            rhs[n, pl.ds(INPUTS, INPUTS), :] = rest[:, n * 128 : n * 128 + 128]

    def turns_of(row, n):
        block = sample[rows_of(row, 256), :]
        return dot(
            jnp.concatenate([block, block], axis=1),
            jnp.concatenate([rhs[2 * n], rhs[2 * n + 1]], axis=1),
        )

    def weights_of(it, side):
        return weights[it, side].reshape(OUTPUTS, BLOCK)

    def make_features(side, base, count, predicting):
        feat = feat_other if side else feat_mine
        shift = phases[side] * (0.5 / math.pi)
        turns_next[...] = turns_of(base, 0)

        def body(i, _):
            tiles = [(m, n) for m in range(2) for n in range(4)]
            now = turns_next[...]
            total = None
            for t, (m, n) in enumerate(tiles):
                row = base + i * 512 + m * 256
                if t + 1 < len(tiles):
                    later = turns_of(base + i * 512 + tiles[t + 1][0] * 256, tiles[t + 1][1])
                else:
                    later = turns_of(base + jnp.minimum(i + 1, count - 1) * 512, 0)
                turn = now + shift[:, n * 256 : n * 256 + 256]
                g = jnp.abs(turn - jnp.round(turn)) - 0.25
                s = g * g
                value = (g * (c1 + s * (c3 + s * (c5 + s * c7)))).astype(BF16)
                rows = rows_of(row, 256)
                feat[2 * n, rows, :] = value[:, :128]
                feat[2 * n + 1, rows, :] = value[:, 128:]
                if predicting:
                    cols = slice(n * 256, n * 256 + 256)
                    before = jnp.concatenate(
                        [feat_mine[2 * n, rows, :], feat_mine[2 * n + 1, rows, :]], axis=1
                    )
                    part = dot_nt(weights_of(0, 0)[:, cols], before)
                    part += dot_nt(weights_of(0, 1)[:, cols], value)
                    total = part if n == 0 else total + part
                    if n == 3:
                        pred[:, rows] = total
                now = later
            turns_next[...] = now
            return 0

        lax.fori_loop(0, count, body, 0)

    with scope("features_mine"):
        make_rhs(0)
        make_features(0, 0, 2, False)

    with scope("barrier"):
        pl.semaphore_wait(barrier, 31)

    om = [
        remote(
            omegas.at[0, pl.ds(0, 64), :],
            omegas.at[1, pl.ds(0, 64), :],
            om_s.at[0],
            om_r.at[0],
            across,
        ),
        remote(
            omegas.at[0, pl.ds(64, 64), :],
            omegas.at[1, pl.ds(64, 64), :],
            om_s.at[1],
            om_r.at[1],
            beside,
        ),
        remote(phases.at[0], phases.at[1], om_s.at[2], om_r.at[2], across),
    ]
    sent = []

    def start(copies):
        for copy in copies:
            copy.start()
        sent.extend(copies)

    start(om)

    def gather(it):
        return [
            remote(
                weights.at[it, 0, y],
                weights.at[it, k // ROWS, y],
                ag_s.at[it, k],
                ag_r.at[it, k],
                chip_device(k),
            )
            for k in range(1, 8)
        ]

    def gather_wait(it, ks):
        for k in ks:
            dx, dy = divmod(k, ROWS)
            came = lax.rem(y + ROWS - dy, ROWS)
            remote(
                weights.at[it, 0, y],
                weights.at[it, dx, came],
                ag_s.at[it, k],
                ag_r.at[it, k],
                chip_device(k),
            ).wait_recv()

    def send_rho(it, rho):
        rhos[it, reg] = jnp.broadcast_to(rho, (1, 128))
        start(
            [
                remote(
                    rhos.at[it, reg], rhos.at[it, reg], ro_s.at[it, k], ro_r.at[it, k], region_device(k)
                )
                for k in range(1, REGIONS)
            ]
        )

    loads[3].wait()
    weights[0, 0, y] = w[...].astype(BF16)
    start(gather(0))
    rho = jnp.full((1, 1), rho_in[0], F32)
    send_rho(0, rho)

    loads[4].wait()
    with scope("features_mine_rest"):
        make_features(0, early, (CHIP - early) // 512, False)

    with scope("omega_wait"):
        for copy in om:
            copy.wait_recv()

    eye = lax.broadcasted_iota(jnp.int32, (128, 128), 0) == lax.broadcasted_iota(
        jnp.int32, (128, 128), 1
    )

    def make_inverse():
        ys, qs, columns, lanes = [], [], [], []
        inv[...] = jnp.zeros_like(inv)
        for b in range(8):
            at = pl.ds(b * 128, 128)
            block = low[at, at]
            diagonal = jnp.where(eye, block, 0.0)
            column = 1.0 / jnp.sum(diagonal, axis=1, keepdims=True)
            lanes.append(1.0 / jnp.sum(diagonal, axis=0, keepdims=True))
            columns.append(column)
            n = jnp.where(eye, 0.0, block) * column
            ys.append(-n)
            qs.append(dot(n.astype(BF16), n.astype(BF16)))
        for step in range(6):
            for b in range(8):
                q = qs[b].astype(BF16)
                if step < 5:
                    both = dot(jnp.concatenate([ys[b].astype(BF16), q], axis=0), q)
                    ys[b] = ys[b] + qs[b] + both[:128]
                    qs[b] = both[128:]
                else:
                    ys[b] = ys[b] + qs[b] + dot(ys[b].astype(BF16), q)
        for b in range(8):
            inv[b, pl.ds(b * 128, 128), :] = ys[b].astype(BF16)

        def square(top, size):
            return jnp.concatenate(
                [inv[top // 128 + i, pl.ds(top, size), :] for i in range(size // 128)], axis=1
            )

        size = 128
        while size < BLOCK:
            for top in range(0, BLOCK, 2 * size):
                column = jnp.concatenate(
                    columns[(top + size) // 128 : (top + 2 * size) // 128], axis=0
                )
                c = low[pl.ds(top + size, size), pl.ds(top, size)] * column
                t = c + dot(square(top + size, size), c.astype(BF16))
                t = (-t - dot(t.astype(BF16), square(top, size))).astype(BF16)
                for i in range(size // 128):
                    inv[top // 128 + i, pl.ds(top + size, size), :] = t[:, i * 128 : i * 128 + 128]
            size *= 2
        return jnp.concatenate(lanes, axis=1)

    def predict(it, side, base, count, more):
        feat = feat_other if side else feat_mine

        def body(i, _):
            for m in range(4):
                rows = rows_of(base + i * 1024 + m * 256, 256)
                block = jnp.concatenate([feat[n, rows, :] for n in range(8)], axis=1)
                part = dot_nt(weights_of(it, side), block)
                pred[:, rows] = pred[:, rows] + part if more else part
            return 0

        lax.fori_loop(0, count, body, 0)

    def scale_to(value, shape):
        return jnp.broadcast_to(value, shape)

    def consensus_send(it, rho):
        value = scale_to(rho, (SLICE, BLOCK)) * (w[...] + u[...])
        for k in range(REGIONS):
            r, c = divmod(k, 8)
            cons_src[it, k] = value[r * 8 : r * 8 + 8, c * 128 : c * 128 + 128]
        cons_sum[it, reg] = cons_src[it, reg]
        start(
            [
                remote(
                    cons_src.at[it, lax.rem(reg + k, REGIONS)],
                    cons_sum.at[it, reg],
                    cs_s.at[it, k],
                    cs_r.at[it, k],
                    region_device(k),
                )
                for k in range(1, REGIONS)
            ]
        )

    def consensus_sum(it):
        with scope("sum_wait"):
            for k in range(1, REGIONS):
                came = lax.rem(reg + REGIONS - k, REGIONS)
                remote(
                    cons_src.at[it, came],
                    cons_sum.at[it, came],
                    cs_s.at[it, k],
                    cs_r.at[it, k],
                    region_device(k),
                ).wait_recv()
                remote(
                    rhos.at[it, came], rhos.at[it, came], ro_s.at[it, k], ro_r.at[it, k], region_device(k)
                ).wait_recv()
        total, divisor = cons_sum[it, 0], rhos[it, 0]
        for k in range(1, REGIONS):
            total = total + cons_sum[it, k]
            divisor = divisor + rhos[it, k]
        cons_all[it, reg] = total / divisor
        start(
            [
                remote(
                    cons_all.at[it, reg],
                    cons_all.at[it, reg],
                    ca_s.at[it, k],
                    ca_r.at[it, k],
                    region_device(k),
                )
                for k in range(1, REGIONS)
            ]
        )

    def consensus_take(it):
        with scope("take_wait"):
            for k in range(1, REGIONS):
                came = lax.rem(reg + REGIONS - k, REGIONS)
                remote(
                    cons_all.at[it, came],
                    cons_all.at[it, came],
                    ca_s.at[it, k],
                    ca_r.at[it, k],
                    region_device(k),
                ).wait_recv()
        gap = jnp.zeros((8, 128), F32)
        drift = jnp.zeros((8, 128), F32)
        for k in range(REGIONS):
            r, c = divmod(k, 8)
            at = (pl.ds(r * 8, 8), pl.ds(c * 128, 128))
            new = cons_all[it, k]
            apart = w[at] - new
            moved = new - z[at]
            gap += apart * apart
            drift += moved * moved
            u[at] = u[at] + apart
            z[at] = new
        row = lax.broadcasted_iota(jnp.int32, (2, 128), 0)
        gap = scale_to(jnp.sum(gap, axis=0, keepdims=True), (2, 128))
        drift = scale_to(jnp.sum(drift, axis=0, keepdims=True), (2, 128))
        me = f * ROWS + y
        gaps[it, me] = jnp.where(row == 0, gap, drift)
        start(
            [
                remote(
                    gaps.at[it, me], gaps.at[it, me], gp_s.at[it, k], gp_r.at[it, k], group_device(k)
                )
                for k in range(1, FEATS * ROWS)
            ]
        )

    def penalty(it, rho):
        with scope("gap_wait"):
            for k in range(1, FEATS * ROWS):
                df, dy = divmod(k, ROWS)
                came = lax.rem(f + FEATS - df, FEATS) * ROWS + lax.rem(y + ROWS - dy, ROWS)
                remote(
                    gaps.at[it, came],
                    gaps.at[it, came],
                    gp_s.at[it, k],
                    gp_r.at[it, k],
                    group_device(k),
                ).wait_recv()
        total = gaps[it, 0]
        for k in range(1, FEATS * ROWS):
            total = total + gaps[it, k]
        total = jnp.sum(total, axis=1, keepdims=True)
        offset = 0.01 * FEATURES * OUTPUTS
        gap, drift = total[0:1], rho * rho * total[1:2]
        new = rho * jnp.sqrt((gap + offset) / (drift + offset))
        u[...] = u[...] * scale_to(rho / new, (SLICE, BLOCK))
        pen_out[:, it : it + 1] = new
        return new

    mine_at = core * HALF
    other_at = (1 - core) * HALF
    lanes = None
    for it in range(ITERS):
        if it == 0:
            with scope("gather_wait"):
                gather_wait(0, range(1, 8))
            with scope("features_other"):
                make_rhs(1)
                make_features(1, other_at, 4, True)
        else:
            with scope("gather_wait"):
                gather_wait(it, range(1, 4))
            with scope("predict_first"):
                predict(it, 0, 0, 4, False)
            with scope("gather_wait"):
                gather_wait(it, range(4, 8))
            with scope("predict_other"):
                predict(it, 1, other_at, 2, True)
        for g in range(HALF // 128):
            pred_send[it, g] = pred[:, rows_of(other_at + g * 128, 128)].astype(BF16)
        to_pair = remote(
            pred_send.at[it], pred_recv.at[it], pair_s.at[it, 0], pair_r.at[it, 0], partner
        )
        start([to_pair])
        if it == 0:
            with scope("features_other_rest"):
                make_features(1, mine_at, 4, True)
            for load in loads[5:]:
                load.wait()
        else:
            consensus_sum(it - 1)
            with scope("predict_mine"):
                predict(it, 1, mine_at, 2, True)
        with scope("pred_wait"):
            to_pair.wait_recv()
        with scope("residual"):
            for g in range(HALF // 128):
                value = pred[:, rows_of(mine_at + g * 128, 128)] + pred_recv[it, g].astype(F32)
                value = value - tgt[:, g * 128 : g * 128 + 128].astype(F32)
                res_own[it, g] = (mem[g : g + 1, :].astype(F32) * value).astype(BF16)
        res = remote(res_own.at[it], res_other.at[it], pair_s.at[it, 1], pair_r.at[it, 1], partner)
        start([res])

        def gradient_part(residual, feat, at, n):
            rows = rows_of(at, HALF)
            return dot(
                jnp.concatenate([residual[it, g] for g in range(HALF // 128)], axis=1),
                jnp.concatenate([feat[2 * n, rows, :], feat[2 * n + 1, rows, :]], axis=1),
            )

        with scope("gradient_mine"):
            for side, feat in ((1, feat_other), (0, feat_mine)):
                for n in range(4):
                    acc[side, :, pl.ds(n * 256, 256)] = gradient_part(res_own, feat, mine_at, n)
        if it:
            consensus_take(it - 1)
        with scope("res_wait"):
            res.wait_recv()
        for side, feat in ((1, feat_other), (0, feat_mine)):
            with scope("gradient_other"):
                for n in range(4):
                    cols = pl.ds(n * 256, 256)
                    total = acc[side, :, cols] + gradient_part(res_other, feat, other_at, n)
                    grad_send[it, side, :, :, cols] = total.reshape(ROWS, SLICE, 256).astype(BF16)
            start(
                [
                    remote(
                        grad_send.at[it, side, chip(k)[1]],
                        grad_recv.at[it, k],
                        rs_s.at[it, k],
                        rs_r.at[it, k],
                        chip_device(k),
                    )
                    for k in range(side * 4, side * 4 + 4)
                    if k
                ]
            )
        if it == 0:
            with scope("inverse"):
                lanes = make_inverse()
        else:
            rho = penalty(it - 1, rho)
            send_rho(it, rho)
        gradient = grad_send[it, 0, y].astype(F32)
        with scope("grad_wait"):
            for k in range(1, 8):
                remote(
                    grad_send.at[it, 0, 0],
                    grad_recv.at[it, k],
                    rs_s.at[it, k],
                    rs_r.at[it, k],
                    chip_device(k),
                ).wait_recv()
        with scope("solve"):
            for k in range(1, 8):
                gradient = gradient + grad_recv[it, k].astype(F32)
            right = gradient + scale_to(rho, (SLICE, BLOCK)) * (w[...] - z[...] + u[...])
            right = right * lanes
            inverse = jnp.concatenate([inv[n] for n in range(8)], axis=1)
            right = right + dot_nt(right.astype(BF16), inverse)
            right = right + dot(right.astype(BF16), inverse)
            new = w[...] - right * lanes
            w[...] = new
        if it < ITERS - 1:
            weights[it + 1, 0, y] = new.astype(BF16)
            start(gather(it + 1))
        with scope("consensus_send"):
            consensus_send(it, rho)

    consensus_sum(ITERS - 1)
    consensus_take(ITERS - 1)
    penalty(ITERS - 1, rho)
    for copy in sent:
        copy.wait_send()


def hand_over(*refs):
    for source, out in zip(refs[:4], refs[4:]):
        out[...] = source[...]


def per_device(
    samples,
    targets,
    member,
    omega,
    phase,
    factors,
    weights_init,
    duals_init,
    consensus_init,
    penalty_init,
):
    hbm = pl.BlockSpec(memory_space=pl.ANY)
    vmem = pl.BlockSpec(memory_space=pltpu.VMEM)
    smem = pl.BlockSpec(memory_space=pltpu.SMEM)
    state = jax.ShapeDtypeStruct((SLICE, BLOCK), F32)
    dma = pltpu.SemaphoreType.DMA
    w, u, z, pen = pl.pallas_call(
        kernel,
        out_shape=(state, state, state, jax.ShapeDtypeStruct((1, ITERS), F32)),
        in_specs=[hbm] * 9 + [smem],
        out_specs=(vmem,) * 4,
        scratch_shapes=[
            pltpu.VMEM((8, CHIP, 128), BF16),
            pltpu.VMEM((8, CHIP, 128), BF16),
            pltpu.VMEM((CHIP, INPUTS), BF16),
            pltpu.VMEM((2, INPUTS, BLOCK), BF16),
            pltpu.VMEM((2, 1, BLOCK), F32),
            pltpu.VMEM((8, 2 * INPUTS, 128), BF16),
            pltpu.VMEM((256, 256), F32),
            pltpu.VMEM((OUTPUTS, HALF), BF16),
            pltpu.VMEM((16, 128), jnp.int32),
            pltpu.VMEM((BLOCK, BLOCK), F32),
            pltpu.VMEM((8, BLOCK, 128), BF16),
            pltpu.VMEM((ITERS, 2, ROWS, SLICE, BLOCK), BF16),
            pltpu.VMEM((OUTPUTS, CHIP), F32),
            pltpu.VMEM((ITERS, 16, OUTPUTS, 128), BF16),
            pltpu.VMEM((ITERS, 16, OUTPUTS, 128), BF16),
            pltpu.VMEM((ITERS, 16, OUTPUTS, 128), BF16),
            pltpu.VMEM((ITERS, 16, OUTPUTS, 128), BF16),
            pltpu.VMEM((2, OUTPUTS, BLOCK), F32),
            pltpu.VMEM((ITERS, 2, ROWS, SLICE, BLOCK), BF16),
            pltpu.VMEM((ITERS, 8, SLICE, BLOCK), BF16),
            pltpu.VMEM((ITERS, REGIONS, 8, 128), F32),
            pltpu.VMEM((ITERS, REGIONS, 8, 128), F32),
            pltpu.VMEM((ITERS, REGIONS, 8, 128), F32),
            pltpu.VMEM((ITERS, REGIONS, 1, 128), F32),
            pltpu.VMEM((ITERS, FEATS * ROWS, 2, 128), F32),
            dma((10,)),
            dma((3,)),
            dma((3,)),
            dma((ITERS, 8)),
            dma((ITERS, 8)),
            dma((ITERS, 8)),
            dma((ITERS, 8)),
            dma((ITERS, 2)),
            dma((ITERS, 2)),
            dma((ITERS, REGIONS)),
            dma((ITERS, REGIONS)),
            dma((ITERS, REGIONS)),
            dma((ITERS, REGIONS)),
            dma((ITERS, REGIONS)),
            dma((ITERS, REGIONS)),
            dma((ITERS, REGIONS)),
            dma((ITERS, REGIONS)),
        ],
        compiler_params=pltpu.CompilerParams(
            collective_id=0, has_side_effects=True, vmem_limit_bytes=60 * 1024 * 1024
        ),
        name="admm",
    )(
        samples,
        targets.T,
        member.reshape(64, 128),
        omega,
        phase.reshape(1, BLOCK),
        factors,
        weights_init.T,
        duals_init.T,
        consensus_init.T,
        penalty_init,
    )
    w, u, z, pen = pl.pallas_call(
        hand_over,
        out_shape=(state, state, state, jax.ShapeDtypeStruct((1, ITERS), F32)),
        in_specs=[vmem] * 4,
        out_specs=(vmem,) * 4,
        name="hand_over",
    )(w, u, z, pen)
    return w.T, u.T, z.T, pen


def solution(mesh):
    return jax.shard_map(
        per_device,
        mesh=mesh,
        in_specs=(
            P(("region", "row"), None),
            P(("region", "row"), None),
            P(("region", "row")),
            P(None, "feat"),
            P("feat"),
            P(("region", "feat"), None),
            P(("region", "feat"), "row"),
            P(("region", "feat"), "row"),
            P("feat", "row"),
            P("region"),
        ),
        out_specs=(
            P(("region", "feat"), "row"),
            P(("region", "feat"), "row"),
            P("feat", "row"),
            P("region", None),
        ),
        check_vma=False,
    )
```

time: 127 us -> 113 us (0.89)
  Pallas kernels: 120 us -> 111 us
  local copies, waits for them, and re-layouts: 5.55 us -> 0 us
    pallas_call x1, Pallas kernels: 120 us -> 110 us  [per_device(): pl.pallas_call(kernel, out_shape=(state, state, state, jax.ShapeDtypeStru...]
    unnamed x4 -> x0, local copies, waits for them, and re-layouts: 5.55 us -> none
    pallas_call x0 -> x1, Pallas kernels: none -> 1.59 us  [per_device(): pl.pallas_call(hand_over, out_shape=(state, state, state, jax.ShapeDtypeS...]
where the time goes in v2:
time: 113 us
  Pallas kernels  111 us (98%)
  between operations  1.29 us (1%)
    pallas_call x1, Pallas kernels, per_device(): pl.pallas_call(kernel, out_shape=(state, state, state, jax.ShapeDtypeStru...  110 us

profile of v2, /device:TPU:1, one launch (start us, length us, event | category | flops | bytes accessed | tf_op | source)
XLA Modules:
  0.0 112.7 jit_solution(16839723105481662094)
XLA Ops:
  1.3 109.8 %admm.1 = (f32[16,1024]{1,0:T(8,128)}, f32[16,1024]{1,0:T(8,128)}, f32[16,1024]{1,0:T(8,128)}, f32[1,3]{1,0:T(1,128)}) custom-call(bf16[8192,128]{1,0:T(8,128)(2,1)} %samples.1, bf16[64,8192]{1,0:T(8,128)(2,1)} %bitcast.9, s32[64,128]{1,0:T(8,128)} %bitcast.13, bf16[128,1024]{1,0:T(8,128)(2,1)} %omega.1, f32[1,1024]{1,0:T(1,128)} %bitcast.14, ...), custom_call_target="tpu_custom_call" | custom-call | tf_op jit(solution)/shard_map/admm/pallas_call | solution.py:628
  111.1 1.6 %hand_over.1 = (f32[16,1024]{1,0:T(8,128)}, f32[16,1024]{1,0:T(8,128)}, f32[16,1024]{1,0:T(8,128)}, f32[1,3]{1,0:T(1,128)}) custom-call(f32[16,1024]{1,0:T(8,128)} %get-tuple-element.12.refs_0_, f32[16,1024]{1,0:T(8,128)} %get-tuple-element.13.refs_1_, f32[16,1024]{1,0:T(8,128)} %get-tuple-element.14.refs_2_, f32[1,3]{1,0:T(1,128)} %get-tuple-element.15.refs_3_), custom_call_target="tpu_custom_call" | custom-call | tf_op jit(solution)/shard_map/hand_over/pallas_call | solution.py:693

commit v3 on v2

--- a/solution.py
+++ b/solution.py
@@ -22,6 +22,7 @@
 F32 = jnp.float32
 BF16 = jnp.bfloat16
 SINE = (6.2831640442521435, -41.33714236464144, 81.34076868066526, -70.99343137755689)
+PIECES = 4
 NT = (((1,), (1,)), ((), ()))
 scope = jax.named_scope
 
@@ -62,6 +63,8 @@
     pen_out,
     feat_mine,
     feat_other,
+    turned_mine,
+    turned_other,
     sample,
     omegas,
     phases,
@@ -71,6 +74,7 @@
     mem,
     low,
     inv,
+    inv_t,
     weights,
     pred,
     pred_send,
@@ -131,7 +135,7 @@
 
     first = xl * CHIP
     half = xl * CHIP + core * HALF
-    early = 1024
+    early = 2048
 
     def rows_of(start, size):
         return pl.ds(pl.multiple_of(start, 128), size)
@@ -193,6 +197,7 @@
 
     def make_features(side, base, count, predicting):
         feat = feat_other if side else feat_mine
+        turned = turned_other if side else turned_mine
         shift = phases[side] * (0.5 / math.pi)
         turns_next[...] = turns_of(base, 0)
 
@@ -206,23 +211,32 @@
                     later = turns_of(base + i * 512 + tiles[t + 1][0] * 256, tiles[t + 1][1])
                 else:
                     later = turns_of(base + jnp.minimum(i + 1, count - 1) * 512, 0)
-                turn = now + shift[:, n * 256 : n * 256 + 256]
-                g = jnp.abs(turn - jnp.round(turn)) - 0.25
-                s = g * g
-                value = (g * (c1 + s * (c3 + s * (c5 + s * c7)))).astype(BF16)
-                rows = rows_of(row, 256)
-                feat[2 * n, rows, :] = value[:, :128]
-                feat[2 * n + 1, rows, :] = value[:, 128:]
+                pieces = []
+                for q in range(PIECES):
+                    size = 256 // PIECES
+                    turn = now[q * size : q * size + size] + shift[:, n * 256 : n * 256 + 256]
+                    g = jnp.abs(turn - jnp.round(turn)) - 0.25
+                    s = g * g
+                    piece = (g * (c1 + s * (c3 + s * (c5 + s * c7)))).astype(BF16)
+                    rows = pl.ds(pl.multiple_of(row + q * size, size), size)
+                    feat[2 * n, rows, :] = piece[:, :128]
+                    feat[2 * n + 1, rows, :] = piece[:, 128:]
+                    pieces.append(piece)
+                value = jnp.concatenate(pieces, axis=0).T
+                cols = pl.ds(n * 256, 256)
+                block = row // 128
+                turned[block, cols, :] = value[:, :128]
+                turned[block + 1, cols, :] = value[:, 128:]
                 if predicting:
-                    cols = slice(n * 256, n * 256 + 256)
+                    some = slice(n * 256, n * 256 + 256)
                     before = jnp.concatenate(
-                        [feat_mine[2 * n, rows, :], feat_mine[2 * n + 1, rows, :]], axis=1
+                        [turned_mine[block, cols, :], turned_mine[block + 1, cols, :]], axis=1
                     )
-                    part = dot_nt(weights_of(0, 0)[:, cols], before)
-                    part += dot_nt(weights_of(0, 1)[:, cols], value)
+                    part = dot(weights_of(0, 0)[:, some], before)
+                    part += dot(weights_of(0, 1)[:, some], value)
                     total = part if n == 0 else total + part
                     if n == 3:
-                        pred[:, rows] = total
+                        pred[:, rows_of(row, 256)] = total
                 now = later
             turns_next[...] = now
             return 0
@@ -231,22 +245,22 @@
 
     with scope("features_mine"):
         make_rhs(0)
-        make_features(0, 0, 2, False)
+        make_features(0, 0, early // 512, False)
 
     with scope("barrier"):
         pl.semaphore_wait(barrier, 31)
 
     om = [
         remote(
-            omegas.at[0, pl.ds(0, 64), :],
-            omegas.at[1, pl.ds(0, 64), :],
+            omegas.at[0, pl.ds(0, 32), :],
+            omegas.at[1, pl.ds(0, 32), :],
             om_s.at[0],
             om_r.at[0],
             across,
         ),
         remote(
-            omegas.at[0, pl.ds(64, 64), :],
-            omegas.at[1, pl.ds(64, 64), :],
+            omegas.at[0, pl.ds(32, 96), :],
+            omegas.at[1, pl.ds(32, 96), :],
             om_s.at[1],
             om_r.at[1],
             beside,
@@ -255,51 +269,67 @@
     ]
     sent = []
 
-    def start(copies):
+    def start(copies, whole, send, recv):
         for copy in copies:
             copy.start()
-        sent.extend(copies)
-
-    start(om)
+        if send is not None:
+            sent.append((whole, send, recv))
+
+    def arrived(whole, send, recv):
+        remote(whole, whole, send, recv, partner).wait_recv()
 
     def gather(it):
-        return [
-            remote(
-                weights.at[it, 0, y],
-                weights.at[it, k // ROWS, y],
-                ag_s.at[it, k],
-                ag_r.at[it, k],
-                chip_device(k),
+        for side, count in ((0, 3), (1, 4)):
+            start(
+                [
+                    remote(
+                        weights.at[it, 0, y],
+                        weights.at[it, side, y],
+                        ag_s.at[it, side],
+                        ag_r.at[it, side],
+                        chip_device(k),
+                    )
+                    for k in range(4 * side + 4 - count, 4 * side + 4)
+                ],
+                weights.at[it, side, pl.ds(0, count)],
+                ag_s.at[it, side],
+                ag_r.at[it, side],
             )
-            for k in range(1, 8)
-        ]
-
-    def gather_wait(it, ks):
-        for k in ks:
-            dx, dy = divmod(k, ROWS)
-            came = lax.rem(y + ROWS - dy, ROWS)
-            remote(
-                weights.at[it, 0, y],
-                weights.at[it, dx, came],
-                ag_s.at[it, k],
-                ag_r.at[it, k],
-                chip_device(k),
-            ).wait_recv()
-
-    def send_rho(it, rho):
-        rhos[it, reg] = jnp.broadcast_to(rho, (1, 128))
+
+    def gather_wait(it, side):
+        arrived(
+            weights.at[it, side, pl.ds(0, 3 + side)], ag_s.at[it, side], ag_r.at[it, side]
+        )
+
+    def to_regions(source, buffer, it, send, recv):
         start(
             [
                 remote(
-                    rhos.at[it, reg], rhos.at[it, reg], ro_s.at[it, k], ro_r.at[it, k], region_device(k)
+                    source(lax.rem(reg + k, REGIONS)),
+                    buffer.at[it, reg],
+                    send.at[it],
+                    recv.at[it],
+                    region_device(k),
                 )
                 for k in range(1, REGIONS)
-            ]
+            ],
+            buffer.at[it, pl.ds(0, REGIONS - 1)],
+            send.at[it],
+            recv.at[it],
         )
+
+    def from_regions(buffer, it, send, recv):
+        arrived(buffer.at[it, pl.ds(0, REGIONS - 1)], send.at[it], recv.at[it])
+
+    def send_rho(it, rho):
+        rhos[it, reg] = jnp.broadcast_to(rho, (1, 128))
+        to_regions(lambda _: rhos.at[it, reg], rhos, it, ro_s, ro_r)
 
     loads[3].wait()
     weights[0, 0, y] = w[...].astype(BF16)
-    start(gather(0))
+    gather(0)
+    for copy in om:
+        copy.start()
     rho = jnp.full((1, 1), rho_in[0], F32)
     send_rho(0, rho)
 
@@ -318,6 +348,7 @@
     def make_inverse():
         ys, qs, columns, lanes = [], [], [], []
         inv[...] = jnp.zeros_like(inv)
+        inv_t[...] = jnp.zeros_like(inv_t)
         for b in range(8):
             at = pl.ds(b * 128, 128)
             block = low[at, at]
@@ -357,20 +388,20 @@
                 for i in range(size // 128):
                     inv[top // 128 + i, pl.ds(top + size, size), :] = t[:, i * 128 : i * 128 + 128]
             size *= 2
+        for r in range(8):
+            for b in range(r + 1):
+                inv_t[r, pl.ds(b * 128, 128), :] = inv[b, pl.ds(r * 128, 128), :].T
         return jnp.concatenate(lanes, axis=1)
 
     def predict(it, side, base, count, more):
-        feat = feat_other if side else feat_mine
-
-        def body(i, _):
-            for m in range(4):
-                rows = rows_of(base + i * 1024 + m * 256, 256)
-                block = jnp.concatenate([feat[n, rows, :] for n in range(8)], axis=1)
-                part = dot_nt(weights_of(it, side), block)
-                pred[:, rows] = pred[:, rows] + part if more else part
-            return 0
-
-        lax.fori_loop(0, count, body, 0)
+        turned = turned_other if side else turned_mine
+        for m in range(count):
+            rows = rows_of(base + m * 256, 256)
+            block = base // 128 + 2 * m
+            part = dot(
+                weights_of(it, side), jnp.concatenate([turned[block], turned[block + 1]], axis=1)
+            )
+            pred[:, rows] = pred[:, rows] + part if more else part
 
     def scale_to(value, shape):
         return jnp.broadcast_to(value, shape)
@@ -381,62 +412,22 @@
             r, c = divmod(k, 8)
             cons_src[it, k] = value[r * 8 : r * 8 + 8, c * 128 : c * 128 + 128]
         cons_sum[it, reg] = cons_src[it, reg]
-        start(
-            [
-                remote(
-                    cons_src.at[it, lax.rem(reg + k, REGIONS)],
-                    cons_sum.at[it, reg],
-                    cs_s.at[it, k],
-                    cs_r.at[it, k],
-                    region_device(k),
-                )
-                for k in range(1, REGIONS)
-            ]
-        )
+        to_regions(lambda r: cons_src.at[it, r], cons_sum, it, cs_s, cs_r)
 
     def consensus_sum(it):
         with scope("sum_wait"):
-            for k in range(1, REGIONS):
-                came = lax.rem(reg + REGIONS - k, REGIONS)
-                remote(
-                    cons_src.at[it, came],
-                    cons_sum.at[it, came],
-                    cs_s.at[it, k],
-                    cs_r.at[it, k],
-                    region_device(k),
-                ).wait_recv()
-                remote(
-                    rhos.at[it, came], rhos.at[it, came], ro_s.at[it, k], ro_r.at[it, k], region_device(k)
-                ).wait_recv()
+            from_regions(cons_sum, it, cs_s, cs_r)
+            from_regions(rhos, it, ro_s, ro_r)
         total, divisor = cons_sum[it, 0], rhos[it, 0]
         for k in range(1, REGIONS):
             total = total + cons_sum[it, k]
             divisor = divisor + rhos[it, k]
         cons_all[it, reg] = total / divisor
-        start(
-            [
-                remote(
-                    cons_all.at[it, reg],
-                    cons_all.at[it, reg],
-                    ca_s.at[it, k],
-                    ca_r.at[it, k],
-                    region_device(k),
-                )
-                for k in range(1, REGIONS)
-            ]
-        )
+        to_regions(lambda _: cons_all.at[it, reg], cons_all, it, ca_s, ca_r)
 
     def consensus_take(it):
         with scope("take_wait"):
-            for k in range(1, REGIONS):
-                came = lax.rem(reg + REGIONS - k, REGIONS)
-                remote(
-                    cons_all.at[it, came],
-                    cons_all.at[it, came],
-                    ca_s.at[it, k],
-                    ca_r.at[it, k],
-                    region_device(k),
-                ).wait_recv()
+            from_regions(cons_all, it, ca_s, ca_r)
         gap = jnp.zeros((8, 128), F32)
         drift = jnp.zeros((8, 128), F32)
         for k in range(REGIONS):
@@ -456,25 +447,17 @@
         gaps[it, me] = jnp.where(row == 0, gap, drift)
         start(
             [
-                remote(
-                    gaps.at[it, me], gaps.at[it, me], gp_s.at[it, k], gp_r.at[it, k], group_device(k)
-                )
+                remote(gaps.at[it, me], gaps.at[it, me], gp_s.at[it], gp_r.at[it], group_device(k))
                 for k in range(1, FEATS * ROWS)
-            ]
+            ],
+            gaps.at[it, pl.ds(0, FEATS * ROWS - 1)],
+            gp_s.at[it],
+            gp_r.at[it],
         )
 
     def penalty(it, rho):
         with scope("gap_wait"):
-            for k in range(1, FEATS * ROWS):
-                df, dy = divmod(k, ROWS)
-                came = lax.rem(f + FEATS - df, FEATS) * ROWS + lax.rem(y + ROWS - dy, ROWS)
-                remote(
-                    gaps.at[it, came],
-                    gaps.at[it, came],
-                    gp_s.at[it, k],
-                    gp_r.at[it, k],
-                    group_device(k),
-                ).wait_recv()
+            arrived(gaps.at[it, pl.ds(0, FEATS * ROWS - 1)], gp_s.at[it], gp_r.at[it])
         total = gaps[it, 0]
         for k in range(1, FEATS * ROWS):
             total = total + gaps[it, k]
@@ -492,34 +475,38 @@
     for it in range(ITERS):
         if it == 0:
             with scope("gather_wait"):
-                gather_wait(0, range(1, 8))
+                gather_wait(0, 0)
+                gather_wait(0, 1)
             with scope("features_other"):
                 make_rhs(1)
                 make_features(1, other_at, 4, True)
         else:
             with scope("gather_wait"):
-                gather_wait(it, range(1, 4))
+                gather_wait(it, 0)
             with scope("predict_first"):
-                predict(it, 0, 0, 4, False)
+                predict(it, 0, 0, 16, False)
+            if it > 1:
+                consensus_sum(it - 1)
             with scope("gather_wait"):
-                gather_wait(it, range(4, 8))
+                gather_wait(it, 1)
             with scope("predict_other"):
-                predict(it, 1, other_at, 2, True)
+                predict(it, 1, other_at, 8, True)
         for g in range(HALF // 128):
             pred_send[it, g] = pred[:, rows_of(other_at + g * 128, 128)].astype(BF16)
         to_pair = remote(
             pred_send.at[it], pred_recv.at[it], pair_s.at[it, 0], pair_r.at[it, 0], partner
         )
-        start([to_pair])
+        start([to_pair], pred_send.at[it], pair_s.at[it, 0], pair_r.at[it, 0])
         if it == 0:
             with scope("features_other_rest"):
                 make_features(1, mine_at, 4, True)
             for load in loads[5:]:
                 load.wait()
         else:
-            consensus_sum(it - 1)
+            if it == 1:
+                consensus_sum(it - 1)
             with scope("predict_mine"):
-                predict(it, 1, mine_at, 2, True)
+                predict(it, 1, mine_at, 8, True)
         with scope("pred_wait"):
             to_pair.wait_recv()
         with scope("residual"):
@@ -528,7 +515,7 @@
                 value = value - tgt[:, g * 128 : g * 128 + 128].astype(F32)
                 res_own[it, g] = (mem[g : g + 1, :].astype(F32) * value).astype(BF16)
         res = remote(res_own.at[it], res_other.at[it], pair_s.at[it, 1], pair_r.at[it, 1], partner)
-        start([res])
+        start([res], res_own.at[it], pair_s.at[it, 1], pair_r.at[it, 1])
 
         def gradient_part(residual, feat, at, n):
             rows = rows_of(at, HALF)
@@ -541,66 +528,95 @@
             for side, feat in ((1, feat_other), (0, feat_mine)):
                 for n in range(4):
                     acc[side, :, pl.ds(n * 256, 256)] = gradient_part(res_own, feat, mine_at, n)
-        if it:
-            consensus_take(it - 1)
         with scope("res_wait"):
             res.wait_recv()
         for side, feat in ((1, feat_other), (0, feat_mine)):
-            with scope("gradient_other"):
-                for n in range(4):
-                    cols = pl.ds(n * 256, 256)
-                    total = acc[side, :, cols] + gradient_part(res_other, feat, other_at, n)
-                    grad_send[it, side, :, :, cols] = total.reshape(ROWS, SLICE, 256).astype(BF16)
-            start(
-                [
-                    remote(
-                        grad_send.at[it, side, chip(k)[1]],
-                        grad_recv.at[it, k],
-                        rs_s.at[it, k],
-                        rs_r.at[it, k],
-                        chip_device(k),
-                    )
-                    for k in range(side * 4, side * 4 + 4)
-                    if k
-                ]
-            )
+            for part in range(2):
+                with scope("gradient_other"):
+                    for n in range(2 * part, 2 * part + 2):
+                        cols = pl.ds(n * 256, 256)
+                        total = acc[side, :, cols] + gradient_part(res_other, feat, other_at, n)
+                        grad_send[it, side, :, :, cols] = total.reshape(ROWS, SLICE, 256).astype(BF16)
+                cols = pl.ds(part * 512, 512)
+                start(
+                    [
+                        remote(
+                            grad_send.at[it, side, chip(k)[1], :, cols],
+                            grad_recv.at[it, k, :, cols],
+                            rs_s.at[it],
+                            rs_r.at[it],
+                            chip_device(k),
+                        )
+                        for k in range(side * 4, side * 4 + 4)
+                        if k
+                    ],
+                    grad_recv.at[it, pl.ds(1, 7)],
+                    rs_s.at[it] if side == 0 and part == 1 else None,
+                    rs_r.at[it],
+                )
         if it == 0:
             with scope("inverse"):
                 lanes = make_inverse()
         else:
-            rho = penalty(it - 1, rho)
-            send_rho(it, rho)
+            consensus_take(it - 1)
+        old_rho_u = scale_to(rho, (SLICE, BLOCK)) * u[...]
         gradient = grad_send[it, 0, y].astype(F32)
         with scope("grad_wait"):
-            for k in range(1, 8):
-                remote(
-                    grad_send.at[it, 0, 0],
-                    grad_recv.at[it, k],
-                    rs_s.at[it, k],
-                    rs_r.at[it, k],
-                    chip_device(k),
-                ).wait_recv()
+            arrived(grad_recv.at[it, pl.ds(1, 7)], rs_s.at[it], rs_r.at[it])
         with scope("solve"):
             for k in range(1, 8):
                 gradient = gradient + grad_recv[it, k].astype(F32)
-            right = gradient + scale_to(rho, (SLICE, BLOCK)) * (w[...] - z[...] + u[...])
+            right = jnp.concatenate([gradient + old_rho_u, w[...] - z[...]], axis=0) * lanes
+            low16 = right.astype(BF16)
+            right = right + jnp.concatenate(
+                [
+                    dot(
+                        low16[:, : n * 256 + 256],
+                        jnp.concatenate(
+                            [inv_t[2 * n + i, pl.ds(0, n * 256 + 256), :] for i in range(2)], axis=1
+                        ),
+                    )
+                    for n in range(4)
+                ],
+                axis=1,
+            )
+            low16 = right.astype(BF16)
+            right = right + jnp.concatenate(
+                [
+                    dot(
+                        low16[:, n * 256 :],
+                        jnp.concatenate(
+                            [
+                                inv[2 * n + i, pl.ds(n * 256, BLOCK - n * 256), :]
+                                for i in range(2)
+                            ],
+                            axis=1,
+                        ),
+                    )
+                    for n in range(4)
+                ],
+                axis=1,
+            )
             right = right * lanes
-            inverse = jnp.concatenate([inv[n] for n in range(8)], axis=1)
-            right = right + dot_nt(right.astype(BF16), inverse)
-            right = right + dot(right.astype(BF16), inverse)
-            new = w[...] - right * lanes
-            w[...] = new
+        if it:
+            rho = penalty(it - 1, rho)
+        new = w[...] - right[:SLICE] - scale_to(rho, (SLICE, BLOCK)) * right[SLICE:]
+        w[...] = new
+        with scope("consensus_send"):
+            consensus_send(it, rho)
         if it < ITERS - 1:
             weights[it + 1, 0, y] = new.astype(BF16)
-            start(gather(it + 1))
-        with scope("consensus_send"):
-            consensus_send(it, rho)
+            gather(it + 1)
+        if it:
+            send_rho(it, rho)
 
     consensus_sum(ITERS - 1)
     consensus_take(ITERS - 1)
     penalty(ITERS - 1, rho)
-    for copy in sent:
+    for copy in om:
         copy.wait_send()
+    for whole, send, recv in sent:
+        remote(whole, whole, send, recv, partner).wait_send()
 
 
 def hand_over(*refs):
@@ -633,6 +649,8 @@
         scratch_shapes=[
             pltpu.VMEM((8, CHIP, 128), BF16),
             pltpu.VMEM((8, CHIP, 128), BF16),
+            pltpu.VMEM((CHIP // 128, BLOCK, 128), BF16),
+            pltpu.VMEM((CHIP // 128, BLOCK, 128), BF16),
             pltpu.VMEM((CHIP, INPUTS), BF16),
             pltpu.VMEM((2, INPUTS, BLOCK), BF16),
             pltpu.VMEM((2, 1, BLOCK), F32),
@@ -641,6 +659,7 @@
             pltpu.VMEM((OUTPUTS, HALF), BF16),
             pltpu.VMEM((16, 128), jnp.int32),
             pltpu.VMEM((BLOCK, BLOCK), F32),
+            pltpu.VMEM((8, BLOCK, 128), BF16),
             pltpu.VMEM((8, BLOCK, 128), BF16),
             pltpu.VMEM((ITERS, 2, ROWS, SLICE, BLOCK), BF16),
             pltpu.VMEM((OUTPUTS, CHIP), F32),
@@ -659,20 +678,20 @@
             dma((10,)),
             dma((3,)),
             dma((3,)),
-            dma((ITERS, 8)),
-            dma((ITERS, 8)),
-            dma((ITERS, 8)),
-            dma((ITERS, 8)),
             dma((ITERS, 2)),
             dma((ITERS, 2)),
-            dma((ITERS, REGIONS)),
-            dma((ITERS, REGIONS)),
-            dma((ITERS, REGIONS)),
-            dma((ITERS, REGIONS)),
-            dma((ITERS, REGIONS)),
-            dma((ITERS, REGIONS)),
-            dma((ITERS, REGIONS)),
-            dma((ITERS, REGIONS)),
+            dma((ITERS,)),
+            dma((ITERS,)),
+            dma((ITERS, 2)),
+            dma((ITERS, 2)),
+            dma((ITERS,)),
+            dma((ITERS,)),
+            dma((ITERS,)),
+            dma((ITERS,)),
+            dma((ITERS,)),
+            dma((ITERS,)),
+            dma((ITERS,)),
+            dma((ITERS,)),
         ],
         compiler_params=pltpu.CompilerParams(
             collective_id=0, has_side_effects=True, vmem_limit_bytes=60 * 1024 * 1024

time: 113 us -> 98.4 us (0.87)
  Pallas kernels: 111 us -> 96.9 us
    pallas_call x1, Pallas kernels: 110 us -> 95.3 us  [per_device(): pl.pallas_call(kernel, out_shape=(state, state, state, jax.ShapeDtypeStru...]
where the time goes in v3:
time: 98.4 us; the launch traced here: 98.2 us
  Pallas kernels  96.9 us (98%)
  between operations  1.29 us (1%)
    pallas_call x1, Pallas kernels, per_device(): pl.pallas_call(kernel, out_shape=(state, state, state, jax.ShapeDtypeStru...  95.3 us

profile of v3, /device:TPU:1, one launch (start us, length us, event | category | flops | bytes accessed | tf_op | source)
XLA Modules:
  0.0 98.2 jit_solution(5516685775057047416)
XLA Ops:
  1.3 95.3 %admm.1 = (f32[16,1024]{1,0:T(8,128)}, f32[16,1024]{1,0:T(8,128)}, f32[16,1024]{1,0:T(8,128)}, f32[1,3]{1,0:T(1,128)}) custom-call(bf16[8192,128]{1,0:T(8,128)(2,1)} %samples.1, bf16[64,8192]{1,0:T(8,128)(2,1)} %bitcast.9, s32[64,128]{1,0:T(8,128)} %bitcast.13, bf16[128,1024]{1,0:T(8,128)(2,1)} %omega.1, f32[1,1024]{1,0:T(1,128)} %bitcast.14, ...), custom_call_target="tpu_custom_call" | custom-call | tf_op jit(solution)/shard_map/admm/pallas_call | solution.py:644
  96.6 1.6 %hand_over.1 = (f32[16,1024]{1,0:T(8,128)}, f32[16,1024]{1,0:T(8,128)}, f32[16,1024]{1,0:T(8,128)}, f32[1,3]{1,0:T(1,128)}) custom-call(f32[16,1024]{1,0:T(8,128)} %get-tuple-element.12.refs_0_, f32[16,1024]{1,0:T(8,128)} %get-tuple-element.13.refs_1_, f32[16,1024]{1,0:T(8,128)} %get-tuple-element.14.refs_2_, f32[1,3]{1,0:T(1,128)} %get-tuple-element.15.refs_3_), custom_call_target="tpu_custom_call" | custom-call | tf_op jit(solution)/shard_map/hand_over/pallas_call | solution.py:712

commit v4 on v3

--- a/solution.py
+++ b/solution.py
@@ -21,7 +21,7 @@
 MESH = pl.DeviceIdType.MESH
 F32 = jnp.float32
 BF16 = jnp.bfloat16
-SINE = (6.2831640442521435, -41.33714236464144, 81.34076868066526, -70.99343137755689)
+SINE = (6.281280070289077, -41.095242279919105, 73.58550951045723)
 PIECES = 4
 NT = (((1,), (1,)), ((), ()))
 scope = jax.named_scope
@@ -175,7 +175,7 @@
             load.wait()
 
     scale = math.sqrt(2.0 / FEATURES)
-    c1, c3, c5, c7 = (-scale * c for c in SINE)
+    c1, c3, c5 = (-scale * c for c in SINE)
 
     def make_rhs(side):
         turns = omegas[side].astype(F32) * (0.5 / math.pi)
@@ -217,7 +217,7 @@
                     turn = now[q * size : q * size + size] + shift[:, n * 256 : n * 256 + 256]
                     g = jnp.abs(turn - jnp.round(turn)) - 0.25
                     s = g * g
-                    piece = (g * (c1 + s * (c3 + s * (c5 + s * c7)))).astype(BF16)
+                    piece = (g * (c1 + s * (c3 + s * c5))).astype(BF16)
                     rows = pl.ds(pl.multiple_of(row + q * size, size), size)
                     feat[2 * n, rows, :] = piece[:, :128]
                     feat[2 * n + 1, rows, :] = piece[:, 128:]

time: 98.4 us -> 96.5 us (0.981)
  Pallas kernels: 96.9 us -> 95.1 us
    pallas_call x1, Pallas kernels: 95.3 us -> 93.5 us  [per_device(): pl.pallas_call(kernel, out_shape=(state, state, state, jax.ShapeDtypeStru...]
where the time goes in v4:
time: 96.5 us; the launch traced here: 96.4 us
  Pallas kernels  95.1 us (99%)
  between operations  1.29 us (1%)
    pallas_call x1, Pallas kernels, per_device(): pl.pallas_call(kernel, out_shape=(state, state, state, jax.ShapeDtypeStru...  93.5 us

profile of v4, /device:TPU:1, one launch (start us, length us, event | category | flops | bytes accessed | tf_op | source)
XLA Modules:
  0.0 96.4 jit_solution(1105656128943690931)
XLA Ops:
  1.3 93.5 %admm.1 = (f32[16,1024]{1,0:T(8,128)}, f32[16,1024]{1,0:T(8,128)}, f32[16,1024]{1,0:T(8,128)}, f32[1,3]{1,0:T(1,128)}) custom-call(bf16[8192,128]{1,0:T(8,128)(2,1)} %samples.1, bf16[64,8192]{1,0:T(8,128)(2,1)} %bitcast.9, s32[64,128]{1,0:T(8,128)} %bitcast.13, bf16[128,1024]{1,0:T(8,128)(2,1)} %omega.1, f32[1,1024]{1,0:T(1,128)} %bitcast.14, ...), custom_call_target="tpu_custom_call" | custom-call | tf_op jit(solution)/shard_map/admm/pallas_call | solution.py:644
  94.8 1.6 %hand_over.1 = (f32[16,1024]{1,0:T(8,128)}, f32[16,1024]{1,0:T(8,128)}, f32[16,1024]{1,0:T(8,128)}, f32[1,3]{1,0:T(1,128)}) custom-call(f32[16,1024]{1,0:T(8,128)} %get-tuple-element.12.refs_0_, f32[16,1024]{1,0:T(8,128)} %get-tuple-element.13.refs_1_, f32[16,1024]{1,0:T(8,128)} %get-tuple-element.14.refs_2_, f32[1,3]{1,0:T(1,128)} %get-tuple-element.15.refs_3_), custom_call_target="tpu_custom_call" | custom-call | tf_op jit(solution)/shard_map/hand_over/pallas_call | solution.py:712

commit v5 on v4

--- a/solution.py
+++ b/solution.py
@@ -23,6 +23,11 @@
 BF16 = jnp.bfloat16
 SINE = (6.281280070289077, -41.095242279919105, 73.58550951045723)
 PIECES = 4
+FAR_REGIONS = sorted(range(1, REGIONS), key=lambda k: -2 * (min(k, REGIONS - k) // 2) - 3 * (k % 2))
+FAR_GROUP = sorted(
+    range(1, FEATS * ROWS), key=lambda k: -min(k % ROWS, ROWS - k % ROWS) - (k // ROWS in (1, 2, 3))
+)
+FAR_CHIPS = ((2, 1, 3), (6, 5, 7, 4))
 NT = (((1,), (1,)), ((), ()))
 scope = jax.named_scope
 
@@ -289,7 +294,7 @@
                         ag_r.at[it, side],
                         chip_device(k),
                     )
-                    for k in range(4 * side + 4 - count, 4 * side + 4)
+                    for k in FAR_CHIPS[side]
                 ],
                 weights.at[it, side, pl.ds(0, count)],
                 ag_s.at[it, side],
@@ -311,7 +316,7 @@
                     recv.at[it],
                     region_device(k),
                 )
-                for k in range(1, REGIONS)
+                for k in FAR_REGIONS
             ],
             buffer.at[it, pl.ds(0, REGIONS - 1)],
             send.at[it],
@@ -448,7 +453,7 @@
         start(
             [
                 remote(gaps.at[it, me], gaps.at[it, me], gp_s.at[it], gp_r.at[it], group_device(k))
-                for k in range(1, FEATS * ROWS)
+                for k in FAR_GROUP
             ],
             gaps.at[it, pl.ds(0, FEATS * ROWS - 1)],
             gp_s.at[it],
@@ -547,8 +552,7 @@
                             rs_r.at[it],
                             chip_device(k),
                         )
-                        for k in range(side * 4, side * 4 + 4)
-                        if k
+                        for k in FAR_CHIPS[side]
                     ],
                     grad_recv.at[it, pl.ds(1, 7)],
                     rs_s.at[it] if side == 0 and part == 1 else None,

time: 96.5 us -> 95 us (0.984)
  Pallas kernels: 95.1 us -> 93.6 us
    pallas_call x1, Pallas kernels: 93.5 us -> 92 us  [per_device(): pl.pallas_call(kernel, out_shape=(state, state, state, jax.ShapeDtypeStru...]
where the time goes in v5:
time: 95 us; the launch traced here: 94.8 us
  Pallas kernels  93.6 us (99%)
  between operations  1.29 us (1%)
    pallas_call x1, Pallas kernels, per_device(): pl.pallas_call(kernel, out_shape=(state, state, state, jax.ShapeDtypeStru...  92 us

profile of v5, /device:TPU:1, one launch (start us, length us, event | category | flops | bytes accessed | tf_op | source)
XLA Modules:
  0.0 94.8 jit_solution(5541802048729897078)
XLA Ops:
  1.3 92.0 %admm.1 = (f32[16,1024]{1,0:T(8,128)}, f32[16,1024]{1,0:T(8,128)}, f32[16,1024]{1,0:T(8,128)}, f32[1,3]{1,0:T(1,128)}) custom-call(bf16[8192,128]{1,0:T(8,128)(2,1)} %samples.1, bf16[64,8192]{1,0:T(8,128)(2,1)} %bitcast.9, s32[64,128]{1,0:T(8,128)} %bitcast.13, bf16[128,1024]{1,0:T(8,128)(2,1)} %omega.1, f32[1,1024]{1,0:T(1,128)} %bitcast.14, ...), custom_call_target="tpu_custom_call" | custom-call | tf_op jit(solution)/shard_map/admm/pallas_call | solution.py:648
  93.3 1.6 %hand_over.1 = (f32[16,1024]{1,0:T(8,128)}, f32[16,1024]{1,0:T(8,128)}, f32[16,1024]{1,0:T(8,128)}, f32[1,3]{1,0:T(1,128)}) custom-call(f32[16,1024]{1,0:T(8,128)} %get-tuple-element.12.refs_0_, f32[16,1024]{1,0:T(8,128)} %get-tuple-element.13.refs_1_, f32[16,1024]{1,0:T(8,128)} %get-tuple-element.14.refs_2_, f32[1,3]{1,0:T(1,128)} %get-tuple-element.15.refs_3_), custom_call_target="tpu_custom_call" | custom-call | tf_op jit(solution)/shard_map/hand_over/pallas_call | solution.py:716
